TPU v7x, 512 devices: a whole 4x8x8 slice. The times are simulated.
512 devices in a mesh: cuts: 32 (over z, y_lo), slab: 16 (over x, y_hi, core).
Axes of the slice: x: 4, y: 8 (y_hi: 2, y_lo: 4; y = y_hi * 4 + y_lo), z: 8, core: 2. Of those that a mesh axis runs over, the one named last changes fastest.
Arguments:
- quasi: bfloat16 [2, 192, 16, 9216], P(None, 'cuts', 'slab'), may hold values from -6 to 6
- counts: int32 [32], replicated, may hold values from 1 to 6, 64 in all
- slot_slice: int32 [192], replicated, may hold values from 0 to 15
- occupation: float32 [192], replicated, may hold values from 0.0078125 to 0.0625
- filter_coef: float32 [16, 9], replicated, may hold values from -2.5 to 2.5
- trap_index: int32 [16, 9216], P('slab'), may hold values from 0 to 31
- trap_table: float32 [32], replicated, may hold values from 0 to 1.5
- mean_field: float32 [16, 9216], P('slab'), may hold values from -1.5 to 0
- pairing: float32 [16, 9216], P('slab'), may hold values from 0.2 to 1
Outputs:
- normal_density: float32 [16, 9216], P('slab', 'cuts')
- anomalous_density: float32 [16, 9216], P('slab', 'cuts')
- new_mean_field: float32 [16, 9216], P('slab', 'cuts')
- new_pairing: float32 [16, 9216], P('slab', 'cuts')
Inputs may be any that keep to these rules, and one draw needn't show every extreme that they name: The live vectors of cut c fill the first counts[c] of its 6 slots; the counts sum to 64 and the largest is exactly 6.
All inputs are finite; a program needn't handle non-finite values.
Results may differ from a plain program's by a relative error of at most 0.0003.
Values may be sent and summed in bfloat16 or wider, within the bound.
No kernel may reach another device: no remote copies, remote signals or barrier semaphores. Data moves between devices by JAX's collectives and lax.ppermute only.
A program may use at most 64 MiB of HBM per device.

v0:
```python
import jax
import jax.numpy as jnp
from jax import lax
from jax.sharding import PartitionSpec as P

NX = 96
VEC_DEV = 2
DEGREE = 8


spectral_scale = 8.5
beta_coef = 0.6
chem_level = 1.0
coupling = 1.0
density_floor = 0.05


def shifted(shard, axis, by):
    devices = lax.axis_size(axis)
    pairs = [(i, i + by) for i in range(devices) if 0 <= i + by < devices]
    return lax.ppermute(shard, axis, pairs)


def combine(field, z_lower, z_upper, y_before, y_after, potential, pairing):
    column = jnp.arange(field.shape[-1]) % NX
    left_ok = (column > 0).astype(jnp.float32)
    right_ok = (column < NX - 1).astype(jnp.float32)
    x_before = jnp.concatenate([jnp.zeros_like(field[..., :1]), field[..., :-1]], axis=3)
    x_after = jnp.concatenate([field[..., 1:], jnp.zeros_like(field[..., :1])], axis=3)
    beside_all = z_lower + z_upper + y_before + y_after
    beside_all = beside_all + x_after * right_ok + x_before * left_ok
    single = 0.5 * (6.0 * field - beside_all) + potential * field
    upper = single[0] + pairing * field[1]
    lower = pairing * field[0] - single[1]
    return jnp.stack([upper, lower]) / spectral_scale


def plane_edges(field):
    below = shifted(field, "slab", 1)
    above = shifted(field, "slab", -1)
    z_lower = jnp.concatenate([below, field[:, :, :-1]], axis=2)
    z_upper = jnp.concatenate([field[:, :, 1:], above], axis=2)
    return (z_lower, z_upper)


def remote_rows(field):
    before = shifted(field[..., -NX:], "cuts", 1)
    after = shifted(field[..., :NX], "cuts", -1)
    y_before = jnp.concatenate([before, field[..., :-NX]], axis=3)
    y_after = jnp.concatenate([field[..., NX:], after], axis=3)
    return (y_before, y_after)


def apply_block(field, potential, pairing, row_source):
    z_lower, z_upper = plane_edges(field)
    y_before, y_after = row_source(field)
    return combine(field, z_lower, z_upper, y_before, y_after, potential, pairing)


def chebyshev(vectors, coefs, operator):
    previous = vectors
    current = operator(vectors)
    filtered = (
        coefs[:, 0][None, :, None, None] * previous + coefs[:, 1][None, :, None, None] * current
    )
    for order in range(2, DEGREE + 1):
        following = 2.0 * operator(current) - previous
        filtered = filtered + coefs[:, order][None, :, None, None] * following
        previous, current = (current, following)
    return filtered


def trap_lookup(index_block, trap_table):
    levels = jnp.arange(trap_table.shape[0])
    onehot = (index_block[:, None, :] == levels[None, :, None]).astype(jnp.float32)
    return jnp.einsum("l,zlf->zf", trap_table, onehot, precision=lax.Precision.HIGHEST)


def slice_coefs(slot_ids, filter_coef):
    levels = jnp.arange(filter_coef.shape[0])
    onehot = (slot_ids[:, None] == levels[None, :]).astype(jnp.float32)
    return jnp.dot(onehot, filter_coef, precision=lax.Precision.HIGHEST)


def body(
    quasi, counts, slot_slice, occupation, filter_coef, trap_index, trap_table, mean_field, pairing
):
    cut_count = lax.axis_size("cuts")
    device = lax.axis_index("cuts")
    cap = quasi.shape[1]
    flat = quasi.shape[3]
    share = flat // cut_count
    offset = device * share
    mean_local = lax.dynamic_slice_in_dim(mean_field, offset, share, 1)
    pairing_local = lax.dynamic_slice_in_dim(pairing, offset, share, 1)
    index_local = lax.dynamic_slice_in_dim(trap_index, offset, share, 1)
    potential = trap_lookup(index_local, trap_table) + mean_local
    moved = lax.all_to_all(quasi, "cuts", split_axis=3, concat_axis=1, tiled=True)
    total_live = VEC_DEV * cut_count
    ends = jnp.cumsum(counts)
    starts = ends - counts
    global_ids = jnp.arange(total_live)
    owner = jnp.sum((ends[None, :] <= global_ids[:, None]).astype(jnp.int32), axis=1)
    owners = jnp.arange(cut_count)
    first = jnp.sum(jnp.where(owners[None, :] == owner[:, None], starts[None, :], 0), axis=1)
    row_ids = owner * cap + global_ids - first
    gathered = jnp.take(moved, row_ids, axis=1).astype(jnp.float32)
    weights = jnp.take(occupation, row_ids)
    coefs = slice_coefs(jnp.take(slot_slice, row_ids), filter_coef)

    def operator(field):
        return apply_block(field, potential, pairing_local, remote_rows)

    filtered = chebyshev(gathered, coefs, operator)
    normal = jnp.sum(weights[:, None, None] * filtered[1] * filtered[1], axis=0)
    anomal = jnp.sum(weights[:, None, None] * filtered[0] * filtered[1], axis=0)
    sums = jnp.stack([normal, anomal])
    normal_density = sums[0]
    anomalous_density = sums[1]
    cube_root = jnp.cbrt(normal_density + density_floor)
    new_mean_field = 0.5 * mean_local + 0.5 * (beta_coef * cube_root * cube_root - chem_level)
    new_pairing = 0.5 * pairing_local - coupling * anomalous_density
    return (normal_density, anomalous_density, new_mean_field, new_pairing)


def solution(mesh):
    return jax.shard_map(
        body,
        mesh=mesh,
        in_specs=(
            P(None, "cuts", "slab", None),
            P(),
            P(),
            P(),
            P(),
            P("slab", None),
            P(),
            P("slab", None),
            P("slab", None),
        ),
        out_specs=(P("slab", "cuts"), P("slab", "cuts"), P("slab", "cuts"), P("slab", "cuts")),
        check_vma=False,
    )
```

profile of v0, /device:TPU:262, one launch (start us, length us, event | category | flops | bytes accessed | tf_op | source)
XLA Modules:
  0.0 266.4 jit_solution(4430877389182085189)
XLA Ops:
  0.7 9.5 %copy.32 = bf16[2,6,1,9216]{1,0,2,3:T(2,128)(2,1)} copy(bf16[2,6,1,9216]{3,0,2,1:T(2,128)(2,1)} %param.9) | data formatting | bytes 442368 | tf_op args[0]
  10.2 11.4 %reshape.1740 = bf16[32,2,1728]{2,1,0:T(2,128)(2,1)} reshape(bf16[9216,1,2,6]{3,2,1,0:T(2,128)(2,1)} %bitcast.79) | data formatting | bytes 442368
  21.6 10.4 %all-to-all-start = ((bf16[32,2,1728]{2,1,0:T(2,128)(2,1)}), bf16[32,2,1728]{2,1,0:T(2,128)(2,1)S(1)}, u32[]{:S(2)}, u32[]{:S(2)}) async-start(bf16[32,2,1728]{2,1,0:T(2,128)(2,1)} %reshape.1740), calls=%async_computation | async-start | bytes 458752 | tf_op jit(solution)/shard_map/all_to_all | solution.py:98
  39.6 11.6 %reshape.1741 = bf16[9216,1,2,6]{3,2,1,0:T(2,128)(2,1)} reshape(bf16[32,2,1728]{2,1,0:T(2,128)(2,1)S(1)} %all-to-all-done) | data formatting | bytes 442368
  51.2 8.7 %copy.36 = bf16[2,6,1,32,288]{4,3,0,1,2:T(8,128)(2,1)S(1)} copy(bf16[2,6,1,32,288]{1,0,4,3,2:T(2,128)(2,1)} %bitcast.78) | data formatting | bytes 442368 | tf_op jit(solution)/shard_map/all_to_all | solution.py:98
  63.4 8.4 %collective-permute-start.1 = (f32[2,64,1,288]{3,0,1,2:T(2,128)S(1)}, f32[2,64,1,288]{3,0,1,2:T(2,128)S(1)}, u32[]{:S(2)}, u32[]{:S(2)}) collective-permute-start(f32[2,64,1,288]{3,0,1,2:T(2,128)S(1)} %fusion.71), channel_id=1, source_target_pairs={{1,0},{2,1},{3,2},{4,3},{5,4},{6,5},{7,6},{8,7},{9,8},{10,9},{11,1... | collective-permute-start | bytes 442376 | tf_op jit(solution)/shard_map/ppermute | solution.py:21
  71.9 5.5 %collective-permute-start.3 = (f32[2,64,1,96]{3,0,1,2:T(2,128)S(1)}, f32[2,64,1,96]{3,0,1,2:T(2,128)S(1)}, u32[]{:S(2)}, u32[]{:S(2)}) collective-permute-start(f32[2,64,1,96]{3,0,1,2:T(2,128)S(1)} %get-tuple-element.67), channel_id=1, source_target_pairs={{16,0},{32,16},{48,32},{64,48},{80,64},{96,80},{112,96},{128,112},... | collective-permute-start | bytes 147464 | tf_op jit(solution)/shard_map/ppermute | solution.py:21
  79.5 7.9 %collective-permute-done.2 = f32[2,64,1,96]{3,0,1,2:T(2,128)S(1)} collective-permute-done((f32[2,64,1,96]{3,0,1,2:T(2,128)S(1)}, f32[2,64,1,96]{3,0,1,2:T(2,128)S(1)}, u32[]{:S(2)}, u32[]{:S(2)}) %collective-permute-start.2) | collective-permute-done | bytes 49184 | tf_op jit(solution)/shard_map/ppermute | solution.py:21
  91.0 8.4 %collective-permute-start.5 = (f32[2,64,1,288]{3,0,1,2:T(2,128)S(1)}, f32[2,64,1,288]{3,0,1,2:T(2,128)S(1)}, u32[]{:S(2)}, u32[]{:S(2)}) collective-permute-start(f32[2,64,1,288]{3,0,1,2:T(2,128)S(1)} %broadcast_multiply_fusion), channel_id=1, source_target_pairs={{1,0},{2,1},{3,2},{4,3},{5,4},{6,5},{7,6},{8,7},{9,8},{10,9},{11,1... | collective-permute-start | bytes 442376 | tf_op jit(solution)/shard_map/ppermute | solution.py:21
  105.6 5.8 %collective-permute-done.6 = f32[2,64,1,96]{3,0,1,2:T(2,128)S(1)} collective-permute-done((f32[2,64,1,96]{3,0,1,2:T(2,128)S(1)}, f32[2,64,1,96]{3,0,1,2:T(2,128)S(1)}, u32[]{:S(2)}, u32[]{:S(2)}) %collective-permute-start.6) | collective-permute-done | bytes 49184 | tf_op jit(solution)/shard_map/ppermute | solution.py:21
  115.1 8.4 %collective-permute-start.9 = (f32[2,64,1,288]{3,0,1,2:T(2,128)S(1)}, f32[2,64,1,288]{3,0,1,2:T(2,128)S(1)}, u32[]{:S(2)}, u32[]{:S(2)}) collective-permute-start(f32[2,64,1,288]{3,0,1,2:T(2,128)S(1)} %fusion.9), channel_id=1, source_target_pairs={{1,0},{2,1},{3,2},{4,3},{5,4},{6,5},{7,6},{8,7},{9,8},{10,9},{11,1... | collective-permute-start | bytes 442376 | tf_op jit(solution)/shard_map/ppermute | solution.py:21
  125.4 4.1 %collective-permute-start.10 = (f32[2,64,1,96]{3,0,1,2:T(2,128)S(1)}, f32[2,64,1,96]{3,0,1,2:T(2,128)S(1)}, u32[]{:S(2)}, u32[]{:S(2)}) collective-permute-start(f32[2,64,1,96]{3,0,1,2:T(2,128)S(1)} %get-tuple-element.54), channel_id=1, source_target_pairs={{0,16},{16,32},{32,48},{48,64},{64,80},{80,96},{96,112},{112,128},... | collective-permute-start | bytes 147464 | tf_op jit(solution)/shard_map/ppermute | solution.py:21
  130.4 5.3 %collective-permute-done.10 = f32[2,64,1,96]{3,0,1,2:T(2,128)S(1)} collective-permute-done((f32[2,64,1,96]{3,0,1,2:T(2,128)S(1)}, f32[2,64,1,96]{3,0,1,2:T(2,128)S(1)}, u32[]{:S(2)}, u32[]{:S(2)}) %collective-permute-start.10) | collective-permute-done | bytes 49184 | tf_op jit(solution)/shard_map/ppermute | solution.py:21
  139.6 8.4 %collective-permute-start.13 = (f32[2,64,1,288]{3,0,1,2:T(2,128)S(1)}, f32[2,64,1,288]{3,0,1,2:T(2,128)S(1)}, u32[]{:S(2)}, u32[]{:S(2)}) collective-permute-start(f32[2,64,1,288]{3,0,1,2:T(2,128)S(1)} %fusion.14), channel_id=1, source_target_pairs={{1,0},{2,1},{3,2},{4,3},{5,4},{6,5},{7,6},{8,7},{9,8},{10,9},{11,1... | collective-permute-start | bytes 442376 | tf_op jit(solution)/shard_map/ppermute | solution.py:21
  154.2 5.8 %collective-permute-done.14 = f32[2,64,1,96]{3,0,1,2:T(2,128)S(1)} collective-permute-done((f32[2,64,1,96]{3,0,1,2:T(2,128)S(1)}, f32[2,64,1,96]{3,0,1,2:T(2,128)S(1)}, u32[]{:S(2)}, u32[]{:S(2)}) %collective-permute-start.14) | collective-permute-done | bytes 49184 | tf_op jit(solution)/shard_map/ppermute | solution.py:21
  164.1 8.4 %collective-permute-start.17 = (f32[2,64,1,288]{3,0,1,2:T(2,128)S(1)}, f32[2,64,1,288]{3,0,1,2:T(2,128)S(1)}, u32[]{:S(2)}, u32[]{:S(2)}) collective-permute-start(f32[2,64,1,288]{3,0,1,2:T(2,128)S(1)} %fusion.19), channel_id=1, source_target_pairs={{1,0},{2,1},{3,2},{4,3},{5,4},{6,5},{7,6},{8,7},{9,8},{10,9},{11,1... | collective-permute-start | bytes 442376 | tf_op jit(solution)/shard_map/ppermute | solution.py:21
  178.7 5.8 %collective-permute-done.18 = f32[2,64,1,96]{3,0,1,2:T(2,128)S(1)} collective-permute-done((f32[2,64,1,96]{3,0,1,2:T(2,128)S(1)}, f32[2,64,1,96]{3,0,1,2:T(2,128)S(1)}, u32[]{:S(2)}, u32[]{:S(2)}) %collective-permute-start.18) | collective-permute-done | bytes 49184 | tf_op jit(solution)/shard_map/ppermute | solution.py:21
  188.9 8.4 %collective-permute-start.21 = (f32[2,64,1,288]{3,0,1,2:T(2,128)S(1)}, f32[2,64,1,288]{3,0,1,2:T(2,128)S(1)}, u32[]{:S(2)}, u32[]{:S(2)}) collective-permute-start(f32[2,64,1,288]{3,0,1,2:T(2,128)S(1)} %fusion.24), channel_id=1, source_target_pairs={{1,0},{2,1},{3,2},{4,3},{5,4},{6,5},{7,6},{8,7},{9,8},{10,9},{11,1... | collective-permute-start | bytes 442376 | tf_op jit(solution)/shard_map/ppermute | solution.py:21
  203.5 5.9 %collective-permute-done.22 = f32[2,64,1,96]{3,0,1,2:T(2,128)S(1)} collective-permute-done((f32[2,64,1,96]{3,0,1,2:T(2,128)S(1)}, f32[2,64,1,96]{3,0,1,2:T(2,128)S(1)}, u32[]{:S(2)}, u32[]{:S(2)}) %collective-permute-start.22) | collective-permute-done | bytes 49184 | tf_op jit(solution)/shard_map/ppermute | solution.py:21
  213.8 8.4 %collective-permute-start.25 = (f32[2,64,1,288]{3,0,1,2:T(2,128)S(1)}, f32[2,64,1,288]{3,0,1,2:T(2,128)S(1)}, u32[]{:S(2)}, u32[]{:S(2)}) collective-permute-start(f32[2,64,1,288]{3,0,1,2:T(2,128)S(1)} %fusion.29), channel_id=1, source_target_pairs={{1,0},{2,1},{3,2},{4,3},{5,4},{6,5},{7,6},{8,7},{9,8},{10,9},{11,1... | collective-permute-start | bytes 442376 | tf_op jit(solution)/shard_map/ppermute | solution.py:21
  224.2 4.1 %collective-permute-start.26 = (f32[2,64,1,96]{3,0,1,2:T(2,128)S(1)}, f32[2,64,1,96]{3,0,1,2:T(2,128)S(1)}, u32[]{:S(2)}, u32[]{:S(2)}) collective-permute-start(f32[2,64,1,96]{3,0,1,2:T(2,128)S(1)} %get-tuple-element.30), channel_id=1, source_target_pairs={{0,16},{16,32},{32,48},{48,64},{64,80},{80,96},{96,112},{112,128},... | collective-permute-start | bytes 147464 | tf_op jit(solution)/shard_map/ppermute | solution.py:21
  228.6 5.8 %collective-permute-done.26 = f32[2,64,1,96]{3,0,1,2:T(2,128)S(1)} collective-permute-done((f32[2,64,1,96]{3,0,1,2:T(2,128)S(1)}, f32[2,64,1,96]{3,0,1,2:T(2,128)S(1)}, u32[]{:S(2)}, u32[]{:S(2)}) %collective-permute-start.26) | collective-permute-done | bytes 49184 | tf_op jit(solution)/shard_map/ppermute | solution.py:21
  239.0 8.4 %collective-permute-start.29 = (f32[2,64,1,288]{3,0,1,2:T(2,128)S(1)}, f32[2,64,1,288]{3,0,1,2:T(2,128)S(1)}, u32[]{:S(2)}, u32[]{:S(2)}) collective-permute-start(f32[2,64,1,288]{3,0,1,2:T(2,128)S(1)} %fusion.34), channel_id=1, source_target_pairs={{1,0},{2,1},{3,2},{4,3},{5,4},{6,5},{7,6},{8,7},{9,8},{10,9},{11,1... | collective-permute-start | bytes 442376 | tf_op jit(solution)/shard_map/ppermute | solution.py:21
  253.7 5.8 %collective-permute-done.30 = f32[2,64,1,96]{3,0,1,2:T(2,128)S(1)} collective-permute-done((f32[2,64,1,96]{3,0,1,2:T(2,128)S(1)}, f32[2,64,1,96]{3,0,1,2:T(2,128)S(1)}, u32[]{:S(2)}, u32[]{:S(2)}) %collective-permute-start.30) | collective-permute-done | bytes 49184 | tf_op jit(solution)/shard_map/ppermute | solution.py:21
  (133 shorter events, 83.8 us)
Async XLA Ops:
  21.6 18.0 %all-to-all-start = ((bf16[32,2,1728]{2,1,0:T(2,128)(2,1)}), bf16[32,2,1728]{2,1,0:T(2,128)(2,1)S(1)}, u32[]{:S(2)}, u32[]{:S(2)}) async-start(bf16[32,2,1728]{2,1,0:T(2,128)(2,1)} %reshape.1740), calls=%async_computation | async-start | bytes 458752 | tf_op jit(solution)/shard_map/all_to_all | solution.py:98
  61.5 25.9 %collective-permute-start = (f32[2,64,1,288]{3,0,1,2:T(2,128)S(1)}, f32[2,64,1,288]{3,0,1,2:T(2,128)S(1)}, u32[]{:S(2)}, u32[]{:S(2)}) collective-permute-start(f32[2,64,1,288]{3,0,1,2:T(2,128)S(1)} %fusion.71), channel_id=1, source_target_pairs={{0,1},{1,2},{2,3},{3,4},{4,5},{5,6},{6,7},{7,8},{8,9},{9,10},{10,1... | collective-permute-start | bytes 442376 | tf_op jit(solution)/shard_map/ppermute | solution.py:21
  63.4 24.0 %collective-permute-start.1 = (f32[2,64,1,288]{3,0,1,2:T(2,128)S(1)}, f32[2,64,1,288]{3,0,1,2:T(2,128)S(1)}, u32[]{:S(2)}, u32[]{:S(2)}) collective-permute-start(f32[2,64,1,288]{3,0,1,2:T(2,128)S(1)} %fusion.71), channel_id=1, source_target_pairs={{1,0},{2,1},{3,2},{4,3},{5,4},{6,5},{7,6},{8,7},{9,8},{10,9},{11,1... | collective-permute-start | bytes 442376 | tf_op jit(solution)/shard_map/ppermute | solution.py:21
  77.4 10.1 %collective-permute-start.2 = (f32[2,64,1,96]{3,0,1,2:T(2,128)S(1)}, f32[2,64,1,96]{3,0,1,2:T(2,128)S(1)}, u32[]{:S(2)}, u32[]{:S(2)}) collective-permute-start(f32[2,64,1,96]{3,0,1,2:T(2,128)S(1)} %get-tuple-element.66), channel_id=1, source_target_pairs={{0,16},{16,32},{32,48},{48,64},{64,80},{80,96},{96,112},{112,128},... | collective-permute-start | bytes 147464 | tf_op jit(solution)/shard_map/ppermute | solution.py:21
  89.1 22.4 %collective-permute-start.4 = (f32[2,64,1,288]{3,0,1,2:T(2,128)S(1)}, f32[2,64,1,288]{3,0,1,2:T(2,128)S(1)}, u32[]{:S(2)}, u32[]{:S(2)}) collective-permute-start(f32[2,64,1,288]{3,0,1,2:T(2,128)S(1)} %broadcast_multiply_fusion), channel_id=1, source_target_pairs={{0,1},{1,2},{2,3},{3,4},{4,5},{5,6},{6,7},{7,8},{8,9},{9,10},{10,1... | collective-permute-start | bytes 442376 | tf_op jit(solution)/shard_map/ppermute | solution.py:21
  91.0 20.5 %collective-permute-start.5 = (f32[2,64,1,288]{3,0,1,2:T(2,128)S(1)}, f32[2,64,1,288]{3,0,1,2:T(2,128)S(1)}, u32[]{:S(2)}, u32[]{:S(2)}) collective-permute-start(f32[2,64,1,288]{3,0,1,2:T(2,128)S(1)} %broadcast_multiply_fusion), channel_id=1, source_target_pairs={{1,0},{2,1},{3,2},{4,3},{5,4},{6,5},{7,6},{8,7},{9,8},{10,9},{11,1... | collective-permute-start | bytes 442376 | tf_op jit(solution)/shard_map/ppermute | solution.py:21
  101.4 10.1 %collective-permute-start.6 = (f32[2,64,1,96]{3,0,1,2:T(2,128)S(1)}, f32[2,64,1,96]{3,0,1,2:T(2,128)S(1)}, u32[]{:S(2)}, u32[]{:S(2)}) collective-permute-start(f32[2,64,1,96]{3,0,1,2:T(2,128)S(1)} %get-tuple-element.60), channel_id=1, source_target_pairs={{0,16},{16,32},{32,48},{48,64},{64,80},{80,96},{96,112},{112,128},... | collective-permute-start | bytes 147464 | tf_op jit(solution)/shard_map/ppermute | solution.py:21
  113.1 22.6 %collective-permute-start.8 = (f32[2,64,1,288]{3,0,1,2:T(2,128)S(1)}, f32[2,64,1,288]{3,0,1,2:T(2,128)S(1)}, u32[]{:S(2)}, u32[]{:S(2)}) collective-permute-start(f32[2,64,1,288]{3,0,1,2:T(2,128)S(1)} %fusion.9), channel_id=1, source_target_pairs={{0,1},{1,2},{2,3},{3,4},{4,5},{5,6},{6,7},{7,8},{8,9},{9,10},{10,1... | collective-permute-start | bytes 442376 | tf_op jit(solution)/shard_map/ppermute | solution.py:21
  115.1 20.6 %collective-permute-start.9 = (f32[2,64,1,288]{3,0,1,2:T(2,128)S(1)}, f32[2,64,1,288]{3,0,1,2:T(2,128)S(1)}, u32[]{:S(2)}, u32[]{:S(2)}) collective-permute-start(f32[2,64,1,288]{3,0,1,2:T(2,128)S(1)} %fusion.9), channel_id=1, source_target_pairs={{1,0},{2,1},{3,2},{4,3},{5,4},{6,5},{7,6},{8,7},{9,8},{10,9},{11,1... | collective-permute-start | bytes 442376 | tf_op jit(solution)/shard_map/ppermute | solution.py:21
  125.4 10.2 %collective-permute-start.10 = (f32[2,64,1,96]{3,0,1,2:T(2,128)S(1)}, f32[2,64,1,96]{3,0,1,2:T(2,128)S(1)}, u32[]{:S(2)}, u32[]{:S(2)}) collective-permute-start(f32[2,64,1,96]{3,0,1,2:T(2,128)S(1)} %get-tuple-element.54), channel_id=1, source_target_pairs={{0,16},{16,32},{32,48},{48,64},{64,80},{80,96},{96,112},{112,128},... | collective-permute-start | bytes 147464 | tf_op jit(solution)/shard_map/ppermute | solution.py:21
  137.7 22.4 %collective-permute-start.12 = (f32[2,64,1,288]{3,0,1,2:T(2,128)S(1)}, f32[2,64,1,288]{3,0,1,2:T(2,128)S(1)}, u32[]{:S(2)}, u32[]{:S(2)}) collective-permute-start(f32[2,64,1,288]{3,0,1,2:T(2,128)S(1)} %fusion.14), channel_id=1, source_target_pairs={{0,1},{1,2},{2,3},{3,4},{4,5},{5,6},{6,7},{7,8},{8,9},{9,10},{10,1... | collective-permute-start | bytes 442376 | tf_op jit(solution)/shard_map/ppermute | solution.py:21
  139.6 20.5 %collective-permute-start.13 = (f32[2,64,1,288]{3,0,1,2:T(2,128)S(1)}, f32[2,64,1,288]{3,0,1,2:T(2,128)S(1)}, u32[]{:S(2)}, u32[]{:S(2)}) collective-permute-start(f32[2,64,1,288]{3,0,1,2:T(2,128)S(1)} %fusion.14), channel_id=1, source_target_pairs={{1,0},{2,1},{3,2},{4,3},{5,4},{6,5},{7,6},{8,7},{9,8},{10,9},{11,1... | collective-permute-start | bytes 442376 | tf_op jit(solution)/shard_map/ppermute | solution.py:21
  150.0 10.1 %collective-permute-start.14 = (f32[2,64,1,96]{3,0,1,2:T(2,128)S(1)}, f32[2,64,1,96]{3,0,1,2:T(2,128)S(1)}, u32[]{:S(2)}, u32[]{:S(2)}) collective-permute-start(f32[2,64,1,96]{3,0,1,2:T(2,128)S(1)} %get-tuple-element.48), channel_id=1, source_target_pairs={{0,16},{16,32},{32,48},{48,64},{64,80},{80,96},{96,112},{112,128},... | collective-permute-start | bytes 147464 | tf_op jit(solution)/shard_map/ppermute | solution.py:21
  162.1 22.4 %collective-permute-start.16 = (f32[2,64,1,288]{3,0,1,2:T(2,128)S(1)}, f32[2,64,1,288]{3,0,1,2:T(2,128)S(1)}, u32[]{:S(2)}, u32[]{:S(2)}) collective-permute-start(f32[2,64,1,288]{3,0,1,2:T(2,128)S(1)} %fusion.19), channel_id=1, source_target_pairs={{0,1},{1,2},{2,3},{3,4},{4,5},{5,6},{6,7},{7,8},{8,9},{9,10},{10,1... | collective-permute-start | bytes 442376 | tf_op jit(solution)/shard_map/ppermute | solution.py:21
  164.1 20.5 %collective-permute-start.17 = (f32[2,64,1,288]{3,0,1,2:T(2,128)S(1)}, f32[2,64,1,288]{3,0,1,2:T(2,128)S(1)}, u32[]{:S(2)}, u32[]{:S(2)}) collective-permute-start(f32[2,64,1,288]{3,0,1,2:T(2,128)S(1)} %fusion.19), channel_id=1, source_target_pairs={{1,0},{2,1},{3,2},{4,3},{5,4},{6,5},{7,6},{8,7},{9,8},{10,9},{11,1... | collective-permute-start | bytes 442376 | tf_op jit(solution)/shard_map/ppermute | solution.py:21
  174.5 10.1 %collective-permute-start.18 = (f32[2,64,1,96]{3,0,1,2:T(2,128)S(1)}, f32[2,64,1,96]{3,0,1,2:T(2,128)S(1)}, u32[]{:S(2)}, u32[]{:S(2)}) collective-permute-start(f32[2,64,1,96]{3,0,1,2:T(2,128)S(1)} %get-tuple-element.42), channel_id=1, source_target_pairs={{0,16},{16,32},{32,48},{48,64},{64,80},{80,96},{96,112},{112,128},... | collective-permute-start | bytes 147464 | tf_op jit(solution)/shard_map/ppermute | solution.py:21
  186.9 22.5 %collective-permute-start.20 = (f32[2,64,1,288]{3,0,1,2:T(2,128)S(1)}, f32[2,64,1,288]{3,0,1,2:T(2,128)S(1)}, u32[]{:S(2)}, u32[]{:S(2)}) collective-permute-start(f32[2,64,1,288]{3,0,1,2:T(2,128)S(1)} %fusion.24), channel_id=1, source_target_pairs={{0,1},{1,2},{2,3},{3,4},{4,5},{5,6},{6,7},{7,8},{8,9},{9,10},{10,1... | collective-permute-start | bytes 442376 | tf_op jit(solution)/shard_map/ppermute | solution.py:21
  188.9 20.6 %collective-permute-start.21 = (f32[2,64,1,288]{3,0,1,2:T(2,128)S(1)}, f32[2,64,1,288]{3,0,1,2:T(2,128)S(1)}, u32[]{:S(2)}, u32[]{:S(2)}) collective-permute-start(f32[2,64,1,288]{3,0,1,2:T(2,128)S(1)} %fusion.24), channel_id=1, source_target_pairs={{1,0},{2,1},{3,2},{4,3},{5,4},{6,5},{7,6},{8,7},{9,8},{10,9},{11,1... | collective-permute-start | bytes 442376 | tf_op jit(solution)/shard_map/ppermute | solution.py:21
  199.2 10.2 %collective-permute-start.22 = (f32[2,64,1,96]{3,0,1,2:T(2,128)S(1)}, f32[2,64,1,96]{3,0,1,2:T(2,128)S(1)}, u32[]{:S(2)}, u32[]{:S(2)}) collective-permute-start(f32[2,64,1,96]{3,0,1,2:T(2,128)S(1)} %get-tuple-element.36), channel_id=1, source_target_pairs={{0,16},{16,32},{32,48},{48,64},{64,80},{80,96},{96,112},{112,128},... | collective-permute-start | bytes 147464 | tf_op jit(solution)/shard_map/ppermute | solution.py:21
  211.9 22.5 %collective-permute-start.24 = (f32[2,64,1,288]{3,0,1,2:T(2,128)S(1)}, f32[2,64,1,288]{3,0,1,2:T(2,128)S(1)}, u32[]{:S(2)}, u32[]{:S(2)}) collective-permute-start(f32[2,64,1,288]{3,0,1,2:T(2,128)S(1)} %fusion.29), channel_id=1, source_target_pairs={{0,1},{1,2},{2,3},{3,4},{4,5},{5,6},{6,7},{7,8},{8,9},{9,10},{10,1... | collective-permute-start | bytes 442376 | tf_op jit(solution)/shard_map/ppermute | solution.py:21
  213.8 20.6 %collective-permute-start.25 = (f32[2,64,1,288]{3,0,1,2:T(2,128)S(1)}, f32[2,64,1,288]{3,0,1,2:T(2,128)S(1)}, u32[]{:S(2)}, u32[]{:S(2)}) collective-permute-start(f32[2,64,1,288]{3,0,1,2:T(2,128)S(1)} %fusion.29), channel_id=1, source_target_pairs={{1,0},{2,1},{3,2},{4,3},{5,4},{6,5},{7,6},{8,7},{9,8},{10,9},{11,1... | collective-permute-start | bytes 442376 | tf_op jit(solution)/shard_map/ppermute | solution.py:21
  224.2 10.2 %collective-permute-start.26 = (f32[2,64,1,96]{3,0,1,2:T(2,128)S(1)}, f32[2,64,1,96]{3,0,1,2:T(2,128)S(1)}, u32[]{:S(2)}, u32[]{:S(2)}) collective-permute-start(f32[2,64,1,96]{3,0,1,2:T(2,128)S(1)} %get-tuple-element.30), channel_id=1, source_target_pairs={{0,16},{16,32},{32,48},{48,64},{64,80},{80,96},{96,112},{112,128},... | collective-permute-start | bytes 147464 | tf_op jit(solution)/shard_map/ppermute | solution.py:21
  237.1 22.4 %collective-permute-start.28 = (f32[2,64,1,288]{3,0,1,2:T(2,128)S(1)}, f32[2,64,1,288]{3,0,1,2:T(2,128)S(1)}, u32[]{:S(2)}, u32[]{:S(2)}) collective-permute-start(f32[2,64,1,288]{3,0,1,2:T(2,128)S(1)} %fusion.34), channel_id=1, source_target_pairs={{0,1},{1,2},{2,3},{3,4},{4,5},{5,6},{6,7},{7,8},{8,9},{9,10},{10,1... | collective-permute-start | bytes 442376 | tf_op jit(solution)/shard_map/ppermute | solution.py:21
  239.0 20.5 %collective-permute-start.29 = (f32[2,64,1,288]{3,0,1,2:T(2,128)S(1)}, f32[2,64,1,288]{3,0,1,2:T(2,128)S(1)}, u32[]{:S(2)}, u32[]{:S(2)}) collective-permute-start(f32[2,64,1,288]{3,0,1,2:T(2,128)S(1)} %fusion.34), channel_id=1, source_target_pairs={{1,0},{2,1},{3,2},{4,3},{5,4},{6,5},{7,6},{8,7},{9,8},{10,9},{11,1... | collective-permute-start | bytes 442376 | tf_op jit(solution)/shard_map/ppermute | solution.py:21
  (15 other events, 260.1 us)
where the time goes:
time: 268 us; the launch traced here: 266 us
  starting transfers between devices  142 us (53%)
  waiting for transfers between devices  52.9 us (20%)
  local copies, waits for them, and re-layouts  50.7 us (19%)
  other arithmetic  18.3 us (7%)
    ppermute x32, starting transfers between devices, shifted(): return lax.ppermute(shard, axis, pairs)  132 us
    ppermute x32, waiting for transfers between devices, shifted(): return lax.ppermute(shard, axis, pairs)  49.5 us
    unnamed x15, local copies, waits for them, and re-layouts  32.5 us
    all_to_all x1, starting transfers between devices, body(): lax.all_to_all(quasi, 'cuts', split_axis=3, concat_axis=1, tiled=True)  10.4 us
    all_to_all x2, local copies, waits for them, and re-layouts, body(): lax.all_to_all(quasi, 'cuts', split_axis=3, concat_axis=1, tiled=True)  8.98 us
    add x8, other arithmetic, combine(): single = 0.5 * (6.0 * field - beside_all) + potential * field  8.3 us
  transfers between devices with their start and end apart: 33, of which 15 were waited for; matrix products, arithmetic and copies ran while one was open for 2% of the time, Pallas kernels for 0%

commit v1 on v0

v1 whole, which is shorter than its diff:
```python
import jax
import jax.numpy as jnp
from jax import lax
from jax.experimental import pallas as pl
from jax.experimental.pallas import tpu as pltpu
from jax.sharding import PartitionSpec as P

NX = 96
DEGREE = 8
CAP = 6
LANES = 128

spectral_scale = 8.5
beta_coef = 0.6
chem_level = 1.0
coupling = 1.0
density_floor = 0.05

PLANES = 16
WINDOWS = 8
TILES = 72
CORE = 9
HALO = 6
SPAN = CORE + 2 * HALO
EXTRA = 6
MESSAGE = SPAN + EXTRA


def pack_kernel(quasi_ref, index_ref, mean_ref, pairing_ref, table_ref, out_ref, rows_ref, pot_ref):
    index = index_ref[...]
    looked = jnp.zeros(index.shape, jnp.float32)
    for level in range(table_ref.shape[0]):
        looked = jnp.where(index == level, table_ref[level], looked)
    potential = looked + mean_ref[...]
    high = potential.astype(jnp.bfloat16).astype(jnp.float32)
    pot_ref[0] = high
    pot_ref[1] = potential - high
    for group in range(2):
        for slot in range(3):
            pair = quasi_ref[3 * group + slot].astype(jnp.float32)
            rows_ref[group, slot : slot + 1, :] = pair[0:1]
            rows_ref[group, 4 + slot : 5 + slot, :] = pair[1:2]
        for tile in range(TILES):
            lanes = slice(tile * LANES, (tile + 1) * LANES)
            rows_ref[group, 3:4, lanes] = pot_ref[0, tile : tile + 1, :]
            rows_ref[group, 7:8, lanes] = pot_ref[1, tile : tile + 1, :]
    for window in range(WINDOWS):
        first = CORE * window - HALO
        begin, end = max(first, 0), min(first + SPAN, TILES)
        for group in range(2):
            slab = 2 * window + group
            if begin > first:
                out_ref[slab, :, : (begin - first) * LANES] = jnp.zeros(
                    (8, (begin - first) * LANES), jnp.bfloat16
                )
            if end < first + SPAN:
                out_ref[slab, :, (end - first) * LANES : SPAN * LANES] = jnp.zeros(
                    (8, (first + SPAN - end) * LANES), jnp.bfloat16
                )
            out_ref[slab, :, (begin - first) * LANES : (end - first) * LANES] = rows_ref[
                group, :, begin * LANES : end * LANES
            ].astype(jnp.bfloat16)
        for extra in range(EXTRA):
            start = first + 4 * extra
            pieces = []
            low, top = max(start, 0), min(start + 4, TILES)
            if low >= top:
                values = jnp.zeros((4, LANES), jnp.float32)
            else:
                values = pairing_ref[low:top, :]
                if low > start:
                    values = jnp.concatenate(
                        [jnp.zeros((low - start, LANES), jnp.float32), values], axis=0
                    )
                if top < start + 4:
                    values = jnp.concatenate(
                        [values, jnp.zeros((start + 4 - top, LANES), jnp.float32)], axis=0
                    )
            upper = values.astype(jnp.bfloat16).astype(jnp.float32)
            tile = jnp.concatenate([upper, values - upper], axis=0).astype(jnp.bfloat16)
            lanes = slice((SPAN + extra) * LANES, (SPAN + extra + 1) * LANES)
            out_ref[2 * window, :, lanes] = tile
            out_ref[2 * window + 1, :, lanes] = tile


def filter_kernel(
    msg_ref, counts_ref, slice_ref, occupation_ref, coef_ref, out_ref, a_ref, c_ref, one_ref, two_ref, acc_ref
):
    cut = lax.axis_index("cuts")
    slab = lax.axis_index("slab")
    group = slab % 2
    window = slab // 2
    row = lax.broadcasted_iota(jnp.int32, (8, LANES), 0)
    lane = lax.broadcasted_iota(jnp.int32, (8, LANES), 1)
    vector = row % 4
    sign = jnp.where(row < 4, 1.0, -1.0).astype(jnp.float32)
    scale = 2.0 / spectral_scale

    base = cut * CAP + group * 3
    coefs = [jnp.zeros((8, LANES), jnp.float32) for _ in range(DEGREE + 1)]
    weight = jnp.zeros((8, LANES), jnp.float32)
    live = counts_ref[cut]
    for slot in range(3):
        mine = vector == slot
        which = slice_ref[base + slot]
        for order in range(DEGREE + 1):
            coefs[order] = jnp.where(mine, coef_ref[which, order], coefs[order])
        alive = jnp.where(group * 3 + slot < live, occupation_ref[base + slot], 0.0)
        weight = jnp.where(mine, alive, weight)

    below_ok = jnp.where(window > 0, 1.0, 0.0)
    above_ok = jnp.where(window < WINDOWS - 1, 1.0, 0.0)

    def inside(tile):
        if tile < HALO:
            return below_ok
        if tile >= HALO + CORE:
            return above_ok
        return None

    hop = sign * (0.5 * scale)
    hops = [hop * below_ok, hop, hop * above_ok]

    def hop_of(tile):
        return hops[0] if tile < HALO else hops[2] if tile >= HALO + CORE else hops[1]

    blank = jnp.zeros((8, SPAN * LANES), jnp.float32)
    for ref in (one_ref, two_ref):
        ref[0] = blank
        ref[PLANES + 1] = blank

    def prepare(z, carry):
        for extra in range(EXTRA):
            fields = msg_ref[z, :, (SPAN + extra) * LANES : (SPAN + extra + 1) * LANES].astype(jnp.float32)
            for part in range(4):
                tile = 4 * extra + part
                if tile >= SPAN:
                    continue
                lanes = slice(tile * LANES, (tile + 1) * LANES)
                block = msg_ref[z, :, lanes].astype(jnp.float32)
                pairing = fields[part : part + 1] + fields[part + 4 : part + 5]
                potential = block[3:4] + block[7:8]
                onsite = (potential + 3.0) * scale
                cross = pairing * scale
                ok = inside(tile)
                if ok is not None:
                    onsite = onsite * ok
                    cross = cross * ok
                a_ref[z, :, lanes] = sign * onsite
                c_ref[z, :, lanes] = jnp.broadcast_to(cross, (8, LANES))
                one_ref[z + 1, :, lanes] = jnp.where(vector < 3, block, 0.0)
        return carry

    lax.fori_loop(0, PLANES, prepare, 0)

    def tile_of(ref, z, tile):
        return ref[z, :, tile * LANES : (tile + 1) * LANES]

    def step(order, current_ref, other_ref):
        first = (96 * order) // LANES
        last = SPAN - 1 - first
        if order == DEGREE:
            first, last = HALO, HALO + CORE - 1

        def plane(z, carry):
            middles, lefts, rights, befores, afters = {}, {}, {}, {}, {}
            for tile in range(max(first - 1, 0), min(last + 1, SPAN - 1) + 1):
                value = tile_of(current_ref, z + 1, tile)
                middles[tile] = value
                lefts[tile] = pltpu.roll(value, 1, 1)
                rights[tile] = pltpu.roll(value, LANES - 1, 1)
                befores[tile] = pltpu.roll(value, 96, 1)
                afters[tile] = pltpu.roll(value, 32, 1)
            for tile in range(first, last + 1):
                previous = max(tile - 1, 0)
                following = min(tile + 1, SPAN - 1)
                kind = tile % 3
                if kind == 0:
                    left = jnp.where((lane == 0) | (lane == 96), 0.0, lefts[tile])
                    right = jnp.where(lane == 127, rights[following], rights[tile])
                    right = jnp.where(lane == 95, 0.0, right)
                elif kind == 1:
                    left = jnp.where(lane == 0, lefts[previous], lefts[tile])
                    left = jnp.where(lane == 64, 0.0, left)
                    right = jnp.where(lane == 127, rights[following], rights[tile])
                    right = jnp.where(lane == 63, 0.0, right)
                else:
                    left = jnp.where(lane == 0, lefts[previous], lefts[tile])
                    left = jnp.where(lane == 32, 0.0, left)
                    right = jnp.where((lane == 31) | (lane == 127), 0.0, rights[tile])
                before = jnp.where(lane < 96, befores[previous], befores[tile])
                after = jnp.where(lane < 32, afters[tile], afters[following])
                beside = (left + right) + (before + after)
                beside = beside + (tile_of(current_ref, z, tile) + tile_of(current_ref, z + 2, tile))
                middle = middles[tile]
                swapped = pltpu.roll(middle, 4, 0)
                result = (
                    tile_of(a_ref, z, tile) * middle
                    + tile_of(c_ref, z, tile) * swapped
                    - hop_of(tile) * beside
                )
                if order == 1:
                    result = 0.5 * result
                else:
                    result = result - tile_of(other_ref, z + 1, tile)
                if order < DEGREE:
                    other_ref[z + 1, :, tile * LANES : (tile + 1) * LANES] = result
                if HALO <= tile < HALO + CORE:
                    core = slice((tile - HALO) * LANES, (tile - HALO + 1) * LANES)
                    if order == 1:
                        total = coefs[0] * middle + coefs[1] * result
                    else:
                        total = acc_ref[z, :, core] + coefs[order] * result
                    if order < DEGREE:
                        acc_ref[z, :, core] = total
                    else:
                        mixed = jnp.where(row < 4, pltpu.roll(total, 4, 0), total) * total
                        mixed = mixed * weight
                        mixed = mixed + pltpu.roll(mixed, 7, 0)
                        mixed = mixed + pltpu.roll(mixed, 6, 0)
                        acc_ref[z, :, core] = mixed
            if order == DEGREE:
                normal = acc_ref[z, 4:5, :]
                anomalous = acc_ref[z, 0:1, :]
                for half in range(2):
                    sites = slice(half * 576, half * 576 + 576)
                    out_ref[2 * z + half, 0:1, :] = normal[:, sites]
                    out_ref[2 * z + half, 1:2, :] = anomalous[:, sites]
            return carry

        lax.fori_loop(0, PLANES, plane, 0)

    for order in range(1, DEGREE + 1):
        if order % 2 == 1:
            step(order, one_ref, two_ref)
        else:
            step(order, two_ref, one_ref)


def sum_kernel(parts_ref, first_ref, second_ref):
    group = lax.axis_index("slab") % 2
    total = jnp.sum(parts_ref[...], axis=0)
    near, far = total[:, :288], total[:, 288:]
    first_ref[...] = jnp.where(group == 0, near, far)
    second_ref[...] = jnp.where(group == 0, far, near)


def vmem(count):
    return [pl.BlockSpec(memory_space=pltpu.VMEM)] * count


def smem(count):
    return [pl.BlockSpec(memory_space=pltpu.SMEM)] * count


def routes(flip):
    pairs = []
    for cut in range(32):
        for slab in range(16):
            group, window = slab % 2, slab // 2
            part = group ^ flip
            pairs.append((cut * 16 + slab, (4 * window + 2 * (cut % 2) + part) * 16 + cut // 2))
    return pairs


def body(
    quasi, counts, slot_slice, occupation, filter_coef, trap_index, trap_table, mean_field, pairing
):
    share = mean_field.shape[1] // lax.axis_size("cuts")
    packed = jnp.transpose(quasi, (1, 2, 0, 3)).reshape(CAP, 2, TILES * LANES)
    message = pl.pallas_call(
        pack_kernel,
        out_shape=jax.ShapeDtypeStruct((PLANES, 8, MESSAGE * LANES), jnp.bfloat16),
        in_specs=vmem(4) + smem(1),
        out_specs=pl.BlockSpec(memory_space=pltpu.VMEM),
        scratch_shapes=[
            pltpu.VMEM((2, 8, TILES * LANES), jnp.float32),
            pltpu.VMEM((2, TILES, LANES), jnp.float32),
        ],
        name="pack",
    )(
        packed,
        trap_index.reshape(TILES, LANES),
        mean_field.reshape(TILES, LANES),
        pairing.reshape(TILES, LANES),
        trap_table,
    )
    message = lax.all_to_all(message, "slab", 0, 0, tiled=True)
    parts = pl.pallas_call(
        filter_kernel,
        out_shape=jax.ShapeDtypeStruct((32, 2, 576), jnp.float32),
        in_specs=vmem(1) + smem(4),
        out_specs=pl.BlockSpec(memory_space=pltpu.VMEM),
        scratch_shapes=[
            pltpu.VMEM((PLANES, 8, SPAN * LANES), jnp.float32),
            pltpu.VMEM((PLANES, 8, SPAN * LANES), jnp.float32),
            pltpu.VMEM((PLANES + 2, 8, SPAN * LANES), jnp.float32),
            pltpu.VMEM((PLANES + 2, 8, SPAN * LANES), jnp.float32),
            pltpu.VMEM((PLANES, 8, CORE * LANES), jnp.float32),
        ],
        name="filter",
    )(message, counts, slot_slice, occupation, filter_coef)
    parts = lax.all_to_all(parts, "cuts", 0, 0, tiled=True)
    first, second = pl.pallas_call(
        sum_kernel,
        out_shape=[jax.ShapeDtypeStruct((2, 288), jnp.float32)] * 2,
        in_specs=vmem(1),
        out_specs=vmem(2),
        name="total",
    )(parts)
    first = lax.ppermute(first, ("cuts", "slab"), routes(0))
    second = lax.ppermute(second, ("cuts", "slab"), routes(1))
    sums = first + second
    offset = lax.axis_index("cuts") * share
    mean_local = lax.dynamic_slice_in_dim(mean_field, offset, share, 1)
    pairing_local = lax.dynamic_slice_in_dim(pairing, offset, share, 1)
    normal_density = sums[0:1]
    anomalous_density = sums[1:2]
    cube_root = jnp.cbrt(normal_density + density_floor)
    new_mean_field = 0.5 * mean_local + 0.5 * (beta_coef * cube_root * cube_root - chem_level)
    new_pairing = 0.5 * pairing_local - coupling * anomalous_density
    return (normal_density, anomalous_density, new_mean_field, new_pairing)


def solution(mesh):
    return jax.shard_map(
        body,
        mesh=mesh,
        in_specs=(
            P(None, "cuts", "slab", None),
            P(),
            P(),
            P(),
            P(),
            P("slab", None),
            P(),
            P("slab", None),
            P("slab", None),
        ),
        out_specs=(P("slab", "cuts"), P("slab", "cuts"), P("slab", "cuts"), P("slab", "cuts")),
        check_vma=False,
    )
```

time: 268 us -> 106 us (0.40)
  the two profiles are of different devices: /device:TPU:262 before, /device:TPU:36 now
where the time goes in v1:
time: 106 us; the launch traced here: 105 us
  blocking collectives  53 us (50%)
  Pallas kernels  26.1 us (25%)
  starting transfers between devices  14.2 us (13%)
  waiting for transfers between devices  10.1 us (10%)
  other arithmetic  1.35 us (1%)
    all_to_all x1, blocking collectives, body(): parts = lax.all_to_all(parts, 'cuts', 0, 0, tiled=True)  28.5 us
    all_to_all x1, blocking collectives, body(): message = lax.all_to_all(message, 'slab', 0, 0, tiled=True)  24.5 us
    pallas_call x1, Pallas kernels, body(): pl.pallas_call(filter_kernel, out_shape=jax.ShapeDtypeStruct((32, 2, 576)...  22.1 us
    ppermute x1, starting transfers between devices, body(): first = lax.ppermute(first, ('cuts', 'slab'), routes(0))  9.11 us
    ppermute x1, waiting for transfers between devices, body(): second = lax.ppermute(second, ('cuts', 'slab'), routes(1))  8.22 us
    ppermute x1, starting transfers between devices, body(): second = lax.ppermute(second, ('cuts', 'slab'), routes(1))  5.05 us
    pallas_call x1, Pallas kernels, body(): pl.pallas_call(pack_kernel, out_shape=jax.ShapeDtypeStruct((PLANES, 8, ME...  2.27 us
  transfers between devices with their start and end apart: 2, of which 2 were waited for; matrix products, arithmetic and copies ran while one was open for 0% of the time, Pallas kernels for 0%

profile of v1, /device:TPU:36, one launch (start us, length us, event | category | flops | bytes accessed | tf_op | source)
XLA Modules:
  0.0 105.4 jit_solution(7604634746159919595)
XLA Ops:
  0.6 2.3 %pack.1 = bf16[16,8,3456]{2,1,0:T(8,128)(2,1)} custom-call(bf16[6,2,9216]{2,1,0:T(2,128)(2,1)} %bitcast.8, s32[72,128]{1,0:T(8,128)} %bitcast.11, f32[72,128]{1,0:T(8,128)} %bitcast.10, f32[72,128]{1,0:T(8,128)} %bitcast.9, f32[32]{0:T(128)} %table_ref.1), custom_call_target="tpu_custom_call" | custom-call | tf_op jit(solution)/shard_map/pack/pallas_call | solution.py:271
  2.9 24.5 %all_to_all.10.msg_ref = bf16[16,8,3456]{2,1,0:T(8,128)(2,1)} all-to-all(bf16[16,8,3456]{2,1,0:T(8,128)(2,1)} %pack.1), channel_id=1, replica_groups=mesh['cuts'=32,'slab'=16] {'slab'}, dimensions={0} | all-to-all | bytes 1769472 | tf_op jit(solution)/shard_map/all_to_all | solution.py:288
  27.4 22.1 %filter.1 = f32[32,2,576]{2,1,0:T(2,128)} custom-call(bf16[16,8,3456]{2,1,0:T(8,128)(2,1)} %all_to_all.10.msg_ref, s32[32]{0:T(128)} %counts_ref.1, s32[192]{0:T(256)} %slice_ref.1, f32[192]{0:T(256)} %occupation_ref.1, f32[16,9]{1,0:T(8,128)} %coef_ref.1), custom_call_target="tpu_custom_call" | custom-call | tf_op jit(solution)/shard_map/filter/pallas_call | solution.py:289
  49.6 28.5 %all_to_all.11.parts_ref = f32[32,2,576]{2,1,0:T(2,128)} all-to-all(f32[32,2,576]{2,1,0:T(2,128)} %filter.1), channel_id=1, replica_groups=mesh['cuts'=32,'slab'=16] {'cuts'}, dimensions={0} | all-to-all | bytes 294912 | tf_op jit(solution)/shard_map/all_to_all | solution.py:303
  78.1 1.7 %total.1 = (f32[2,288]{1,0:T(2,128)}, f32[2,288]{1,0:T(2,128)}) custom-call(f32[32,2,576]{2,1,0:T(2,128)} %all_to_all.11.parts_ref), custom_call_target="tpu_custom_call" | custom-call | tf_op jit(solution)/shard_map/total/pallas_call | solution.py:304
  79.8 0.0 copy-start
  79.8 9.1 %collective-permute-start = (f32[2,288]{1,0:T(2,128)}, f32[2,288]{1,0:T(2,128)S(1)}, u32[]{:S(2)}, u32[]{:S(2)}) collective-permute-start(f32[2,288]{1,0:T(2,128)} %get-tuple-element.6), channel_id=1, source_target_pairs={{0,0},{1,16},{2,64},{3,80},{4,128},{5,144},{6,192},{7,208},{8,256}... | collective-permute-start | bytes 6920 | tf_op jit(solution)/shard_map/ppermute | solution.py:311
  88.9 0.0 copy-done
  88.9 5.0 %collective-permute-start.1 = (f32[2,288]{1,0:T(2,128)S(1)}, f32[2,288]{1,0:T(2,128)S(1)}, u32[]{:S(2)}, u32[]{:S(2)}) collective-permute-start(f32[2,288]{1,0:T(2,128)S(1)} %copy-done), channel_id=1, source_target_pairs={{0,16},{1,0},{2,80},{3,64},{4,144},{5,128},{6,208},{7,192},{8,272}... | collective-permute-start | bytes 6920 | tf_op jit(solution)/shard_map/ppermute | solution.py:312
  94.0 1.9 %collective-permute-done = f32[2,288]{1,0:T(2,128)S(1)} collective-permute-done((f32[2,288]{1,0:T(2,128)}, f32[2,288]{1,0:T(2,128)S(1)}, u32[]{:S(2)}, u32[]{:S(2)}) %collective-permute-start) | collective-permute-done | bytes 2336 | tf_op jit(solution)/shard_map/ppermute | solution.py:311
  95.8 8.2 %collective-permute-done.1 = f32[2,288]{1,0:T(2,128)S(1)} collective-permute-done((f32[2,288]{1,0:T(2,128)S(1)}, f32[2,288]{1,0:T(2,128)S(1)}, u32[]{:S(2)}, u32[]{:S(2)}) %collective-permute-start.1) | collective-permute-done | bytes 2336 | tf_op jit(solution)/shard_map/ppermute | solution.py:312
  104.0 1.3 %multiply_subtract_fusion = (f32[1,288]{1,0:T(1,128)}, f32[1,288]{1,0:T(1,128)}, f32[1,288]{1,0:T(1,128)}, f32[1,288]{1,0:T(1,128)}) fusion(f32[1,9216]{1,0:T(1,128)} %param.17, s32[]{:T(128)S(6)} %select_n.4, f32[2,288]{1,0:T(2,128)S(1)} %add.18, f32[1,9216]{1,0:T(1,128)} %param.16), kind=kLoop, calls=%fused_computation.3 | loop fusion | flops 2304 | bytes 9220 | tf_op jit(solution)/shard_map/sub | solution.py:321
  (1 shorter events, 0.0 us)
Async XLA Ops:
  79.8 9.1 %copy-start = (f32[2,288]{1,0:T(2,128)S(1)}, f32[2,288]{1,0:T(2,128)}, u32[]{:S(2)}) copy-start(f32[2,288]{1,0:T(2,128)} %get-tuple-element.7) | copy-start | bytes 6916
  79.8 16.0 %collective-permute-start = (f32[2,288]{1,0:T(2,128)}, f32[2,288]{1,0:T(2,128)S(1)}, u32[]{:S(2)}, u32[]{:S(2)}) collective-permute-start(f32[2,288]{1,0:T(2,128)} %get-tuple-element.6), channel_id=1, source_target_pairs={{0,0},{1,16},{2,64},{3,80},{4,128},{5,144},{6,192},{7,208},{8,256}... | collective-permute-start | bytes 6920 | tf_op jit(solution)/shard_map/ppermute | solution.py:311
  88.9 15.1 %collective-permute-start.1 = (f32[2,288]{1,0:T(2,128)S(1)}, f32[2,288]{1,0:T(2,128)S(1)}, u32[]{:S(2)}, u32[]{:S(2)}) collective-permute-start(f32[2,288]{1,0:T(2,128)S(1)} %copy-done), channel_id=1, source_target_pairs={{0,16},{1,0},{2,80},{3,64},{4,144},{5,128},{6,208},{7,192},{8,272}... | collective-permute-start | bytes 6920 | tf_op jit(solution)/shard_map/ppermute | solution.py:312

commit v2 on v1

v2 whole, which is shorter than its diff:
```python
import jax
import jax.numpy as jnp
from jax import lax
from jax.experimental import pallas as pl
from jax.experimental.pallas import tpu as pltpu
from jax.sharding import PartitionSpec as P

NX = 96
DEGREE = 8
CAP = 6
LANES = 128

spectral_scale = 8.5
beta_coef = 0.6
chem_level = 1.0
coupling = 1.0
density_floor = 0.05

PLANES = 16
WINDOWS = 8
TILES = 72
CORE = 9
HALO = 6
SPAN = CORE + 2 * HALO
EXTRA = 6
MESSAGE = SPAN + EXTRA


def pack_kernel(quasi_ref, index_ref, mean_ref, pairing_ref, table_ref, out_ref, rows_ref, pot_ref):
    index = index_ref[...]
    looked = jnp.zeros(index.shape, jnp.float32)
    for level in range(table_ref.shape[0]):
        looked = jnp.where(index == level, table_ref[level], looked)
    potential = looked + mean_ref[...]
    high = potential.astype(jnp.bfloat16).astype(jnp.float32)
    pot_ref[0] = high
    pot_ref[1] = potential - high
    for group in range(2):
        for slot in range(3):
            pair = quasi_ref[3 * group + slot].astype(jnp.float32)
            rows_ref[group, slot : slot + 1, :] = pair[0:1]
            rows_ref[group, 4 + slot : 5 + slot, :] = pair[1:2]
        for tile in range(TILES):
            lanes = slice(tile * LANES, (tile + 1) * LANES)
            rows_ref[group, 3:4, lanes] = pot_ref[0, tile : tile + 1, :]
            rows_ref[group, 7:8, lanes] = pot_ref[1, tile : tile + 1, :]
    for window in range(WINDOWS):
        first = CORE * window - HALO
        begin, end = max(first, 0), min(first + SPAN, TILES)
        for group in range(2):
            slab = 2 * window + group
            if begin > first:
                out_ref[slab, :, : (begin - first) * LANES] = jnp.zeros(
                    (8, (begin - first) * LANES), jnp.bfloat16
                )
            if end < first + SPAN:
                out_ref[slab, :, (end - first) * LANES : SPAN * LANES] = jnp.zeros(
                    (8, (first + SPAN - end) * LANES), jnp.bfloat16
                )
            out_ref[slab, :, (begin - first) * LANES : (end - first) * LANES] = rows_ref[
                group, :, begin * LANES : end * LANES
            ].astype(jnp.bfloat16)
        for extra in range(EXTRA):
            start = first + 4 * extra
            pieces = []
            low, top = max(start, 0), min(start + 4, TILES)
            if low >= top:
                values = jnp.zeros((4, LANES), jnp.float32)
            else:
                values = pairing_ref[low:top, :]
                if low > start:
                    values = jnp.concatenate(
                        [jnp.zeros((low - start, LANES), jnp.float32), values], axis=0
                    )
                if top < start + 4:
                    values = jnp.concatenate(
                        [values, jnp.zeros((start + 4 - top, LANES), jnp.float32)], axis=0
                    )
            upper = values.astype(jnp.bfloat16).astype(jnp.float32)
            tile = jnp.concatenate([upper, values - upper], axis=0).astype(jnp.bfloat16)
            lanes = slice((SPAN + extra) * LANES, (SPAN + extra + 1) * LANES)
            out_ref[2 * window, :, lanes] = tile
            out_ref[2 * window + 1, :, lanes] = tile


ROWS = 28
OWN = 12
STRIDE = 24
BLOCK = ROWS * STRIDE


def filter_kernel(
    msg_ref, counts_ref, slice_ref, occupation_ref, coef_ref, keep_ref, send_ref,
    one_ref, two_ref, a_ref, c_ref, acc_ref, density_ref,
):
    cut = lax.axis_index("cuts")
    slab = lax.axis_index("slab")
    group = slab % 2
    window = slab // 2
    scale = 2.0 / spectral_scale
    lane = lax.broadcasted_iota(jnp.int32, (8, LANES), 1)
    below_ok = jnp.where(window > 0, 1.0, 0.0)
    above_ok = jnp.where(window < WINDOWS - 1, 1.0, 0.0)
    on_row = jnp.where(lane < NX, 1.0, 0.0).astype(jnp.float32)
    inside = [on_row * below_ok, on_row, on_row * above_ok]

    def place(y):
        return 0 if y < 8 else 1 if y < 8 + OWN else 2

    hops = [mask * (0.5 * scale) for mask in inside]

    def chosen(count, pick):
        out = lax.broadcasted_iota(jnp.int32, (count, LANES), 0)
        source = lax.broadcasted_iota(jnp.int32, (count, LANES), 1)
        same = (out % PLANES) == (source // 8)
        return jnp.where(same & pick(out // PLANES, source % 8), 1.0, 0.0).astype(jnp.bfloat16)

    gather = chosen(
        7 * PLANES,
        lambda i, row: (row == (i // 3) * 4 + i % 3) | ((i == 6) & (row % 4 == 3)),
    )
    spread = chosen(4 * PLANES, lambda part, row: row % 4 == part)

    for ref in (one_ref, two_ref):
        for block in range(6 * ROWS + 1):
            ref[block * STRIDE : block * STRIDE + 8, :] = jnp.zeros((8, LANES), jnp.float32)
    density_ref[...] = jnp.zeros_like(density_ref)

    def unpack(tiles):
        first, second, third = tiles
        wide = lax.broadcasted_iota(jnp.int32, first.shape, 1)
        ok = wide < NX
        rows = [
            first,
            jnp.where(wide < 32, pltpu.roll(first, 32, 1), pltpu.roll(second, 32, 1)),
            jnp.where(wide < 64, pltpu.roll(second, 64, 1), pltpu.roll(third, 64, 1)),
            pltpu.roll(third, 96, 1),
        ]
        return [jnp.where(ok, row, 0.0) for row in rows]

    fields = []
    for extra in range(EXTRA):
        lanes = slice((SPAN + extra) * LANES, (SPAN + extra + 1) * LANES)
        part = jnp.dot(spread, msg_ref[:, lanes], preferred_element_type=jnp.float32)
        fields += [part[16 * k : 16 * k + 16] for k in range(4)]
    for quad in range(ROWS // 4):
        lanes = slice(3 * quad * LANES, 3 * (quad + 1) * LANES)
        taken = jnp.dot(gather, msg_ref[:, lanes], preferred_element_type=jnp.float32)
        rows = unpack([taken[:, k * LANES : (k + 1) * LANES] for k in range(3)])
        pairs = unpack(fields[3 * quad : 3 * quad + 3])
        for k in range(4):
            y = 4 * quad + k
            mask = inside[place(y)]
            for i in range(6):
                base = i * BLOCK + y * STRIDE + 8
                one_ref[base : base + 16, :] = rows[k][16 * i : 16 * i + 16]
            for high in range(2):
                at = slice(16 * y + 8 * high, 16 * y + 8 * high + 8)
                a_ref[at, :] = (rows[k][96 + 8 * high : 104 + 8 * high] + 3.0) * (mask * scale)
                c_ref[at, :] = pairs[k][8 * high : 8 * high + 8] * (mask * scale)

    live = counts_ref[cut]
    start = cut * CAP + group * 3

    def vector(slot, carry):
        which = slice_ref[start + slot]
        weight = jnp.where(group * 3 + slot < live, occupation_ref[start + slot], 0.0)
        coefs = [coef_ref[which, order] for order in range(DEGREE + 1)]
        shift = slot * BLOCK

        def load(ref, comp, y, offset):
            origin = pl.multiple_of(shift + comp * 3 * BLOCK, 8)
            return ref[pl.ds(origin + y * STRIDE + 8 + offset, 8), :]

        for order in range(1, DEGREE + 1):
            now, other = (one_ref, two_ref) if order % 2 == 1 else (two_ref, one_ref)
            for y in range(order, ROWS - order):
                hop = hops[place(y)]
                for high in range(2):
                    z = 8 * high
                    onsite = a_ref[16 * y + z : 16 * y + z + 8, :]
                    cross = c_ref[16 * y + z : 16 * y + z + 8, :]
                    middles, singles = [], []
                    for comp in range(2):
                        middle = load(now, comp, y, z)
                        beside = pltpu.roll(middle, 1, 1) + pltpu.roll(middle, LANES - 1, 1)
                        beside = beside + (load(now, comp, y - 1, z) + load(now, comp, y + 1, z))
                        beside = beside + (load(now, comp, y, z - 1) + load(now, comp, y, z + 1))
                        middles.append(middle)
                        singles.append(onsite * middle - hop * beside)
                    results = [
                        singles[0] + cross * middles[1],
                        cross * middles[0] - singles[1],
                    ]
                    totals = []
                    for comp in range(2):
                        result = results[comp]
                        if order == 1:
                            result = 0.5 * result
                        else:
                            result = result - load(other, comp, y, z)
                        if order < DEGREE:
                            origin = pl.multiple_of(shift + comp * 3 * BLOCK, 8)
                            other[pl.ds(origin + y * STRIDE + 8 + z, 8), :] = result
                        if 8 <= y < 8 + OWN:
                            at = (comp * OWN + y - 8) * 16 + z
                            if order == 1:
                                total = coefs[0] * middles[comp] + coefs[1] * result
                            else:
                                total = acc_ref[at : at + 8, :] + coefs[order] * result
                            if order < DEGREE:
                                acc_ref[at : at + 8, :] = total
                            totals.append(total)
                    if order == DEGREE:
                        weighted = weight * totals[1]
                        at = (y - 8) * 16 + z
                        density_ref[at : at + 8, :] += weighted * totals[1]
                        at = at + OWN * 16
                        density_ref[at : at + 8, :] += weighted * totals[0]
        return carry

    lax.fori_loop(0, 3, vector, 0)

    for density in range(2):
        for y in range(OWN):
            quarter, row = y // 3, y % 3
            lanes = slice((3 * density + row) * LANES, (3 * density + row + 1) * LANES)
            at = (density * OWN + y) * 16
            first, second = density_ref[at : at + 8, :], density_ref[at + 8 : at + 16, :]
            mine = group == 0
            keep_ref[8 * quarter : 8 * quarter + 8, lanes] = jnp.where(mine, first, second)
            send_ref[8 * quarter : 8 * quarter + 8, lanes] = jnp.where(mine, second, first)


def join_kernel(keep_ref, got_ref, out_ref):
    total = keep_ref[...] + got_ref[...]
    for piece in range(32):
        out_ref[piece] = total[piece : piece + 1]


def sum_kernel(parts_ref, out_ref):
    total = jnp.sum(parts_ref[...], axis=0)
    lane = lax.broadcasted_iota(jnp.int32, (1, LANES), 1)
    for density in range(2):
        first, second, third = [
            total[:, (3 * density + k) * LANES : (3 * density + k + 1) * LANES] for k in range(3)
        ]
        second, third = pltpu.roll(second, 96, 1), pltpu.roll(third, 64, 1)
        row = slice(density, density + 1)
        out_ref[row, 0:128] = jnp.where(lane < 96, first, second)
        out_ref[row, 128:256] = jnp.where(lane < 64, second, third)
        out_ref[row, 256:288] = third[:, :32]


def vmem(count):
    return [pl.BlockSpec(memory_space=pltpu.VMEM)] * count


def smem(count):
    return [pl.BlockSpec(memory_space=pltpu.SMEM)] * count


def filter_call(message, counts, slot_slice, occupation, filter_coef):
    return pl.pallas_call(
        filter_kernel,
        out_shape=[jax.ShapeDtypeStruct((32, 6 * LANES), jnp.float32)] * 2,
        in_specs=vmem(1) + smem(4),
        out_specs=vmem(2),
        scratch_shapes=[
            pltpu.VMEM((6 * BLOCK + 8, LANES), jnp.float32),
            pltpu.VMEM((6 * BLOCK + 8, LANES), jnp.float32),
            pltpu.VMEM((16 * ROWS, LANES), jnp.float32),
            pltpu.VMEM((16 * ROWS, LANES), jnp.float32),
            pltpu.VMEM((2 * OWN * 16, LANES), jnp.float32),
            pltpu.VMEM((2 * OWN * 16, LANES), jnp.float32),
        ],
        name="filter",
    )(message.reshape(8 * PLANES, MESSAGE * LANES), counts, slot_slice, occupation, filter_coef)


def partners():
    return [(slab, slab ^ 1) for slab in range(16)]


def routes():
    pairs = []
    for cut in range(32):
        for slab in range(16):
            group, window = slab % 2, slab // 2
            target = (4 * window + cut // 8) * 16 + 8 * group + cut % 8
            pairs.append((cut * 16 + slab, target))
    return pairs


def body(
    quasi, counts, slot_slice, occupation, filter_coef, trap_index, trap_table, mean_field, pairing
):
    share = mean_field.shape[1] // lax.axis_size("cuts")
    packed = jnp.transpose(quasi, (1, 2, 0, 3)).reshape(CAP, 2, TILES * LANES)
    message = pl.pallas_call(
        pack_kernel,
        out_shape=jax.ShapeDtypeStruct((PLANES, 8, MESSAGE * LANES), jnp.bfloat16),
        in_specs=vmem(4) + smem(1),
        out_specs=pl.BlockSpec(memory_space=pltpu.VMEM),
        scratch_shapes=[
            pltpu.VMEM((2, 8, TILES * LANES), jnp.float32),
            pltpu.VMEM((2, TILES, LANES), jnp.float32),
        ],
        name="pack",
    )(
        packed,
        trap_index.reshape(TILES, LANES),
        mean_field.reshape(TILES, LANES),
        pairing.reshape(TILES, LANES),
        trap_table,
    )
    message = lax.all_to_all(message, "slab", 0, 0, tiled=True)
    keep, send = filter_call(message, counts, slot_slice, occupation, filter_coef)
    got = lax.ppermute(send, "slab", partners())
    parts = pl.pallas_call(
        join_kernel,
        out_shape=jax.ShapeDtypeStruct((32, 1, 6 * LANES), jnp.float32),
        in_specs=vmem(2),
        out_specs=pl.BlockSpec(memory_space=pltpu.VMEM),
        name="join",
    )(keep, got)
    parts = lax.all_to_all(parts, "cuts", 0, 0, tiled=True)
    sums = pl.pallas_call(
        sum_kernel,
        out_shape=jax.ShapeDtypeStruct((2, 288), jnp.float32),
        in_specs=vmem(1),
        out_specs=pl.BlockSpec(memory_space=pltpu.VMEM),
        name="total",
    )(parts)
    sums = lax.ppermute(sums, ("cuts", "slab"), routes())
    offset = lax.axis_index("cuts") * share
    mean_local = lax.dynamic_slice_in_dim(mean_field, offset, share, 1)
    pairing_local = lax.dynamic_slice_in_dim(pairing, offset, share, 1)
    normal_density = sums[0:1]
    anomalous_density = sums[1:2]
    cube_root = jnp.cbrt(normal_density + density_floor)
    new_mean_field = 0.5 * mean_local + 0.5 * (beta_coef * cube_root * cube_root - chem_level)
    new_pairing = 0.5 * pairing_local - coupling * anomalous_density
    return (normal_density, anomalous_density, new_mean_field, new_pairing)


def solution(mesh):
    return jax.shard_map(
        body,
        mesh=mesh,
        in_specs=(
            P(None, "cuts", "slab", None),
            P(),
            P(),
            P(),
            P(),
            P("slab", None),
            P(),
            P("slab", None),
            P("slab", None),
        ),
        out_specs=(P("slab", "cuts"), P("slab", "cuts"), P("slab", "cuts"), P("slab", "cuts")),
        check_vma=False,
    )
```

time: 106 us -> 88.3 us (0.83)
  the two profiles are of different devices: /device:TPU:36 before, /device:TPU:16 now
where the time goes in v2:
time: 88.3 us; the launch traced here: 87.9 us
  blocking collectives  57.4 us (65%)
  Pallas kernels  13.1 us (15%)
  waiting for transfers between devices  10.8 us (12%)
  starting transfers between devices  3.92 us (4%)
  other arithmetic  1.34 us (2%)
    all_to_all x1, blocking collectives, body(): message = lax.all_to_all(message, 'slab', 0, 0, tiled=True)  36 us
    all_to_all x1, blocking collectives, body(): parts = lax.all_to_all(parts, 'cuts', 0, 0, tiled=True)  21.4 us
    ppermute x1, waiting for transfers between devices, body(): sums = lax.ppermute(sums, ('cuts', 'slab'), routes())  9.37 us
    pallas_call x1, Pallas kernels, filter_call(): pl.pallas_call(filter_kernel, out_shape=[jax.ShapeDtypeStruct((32, 6 * LA...  7.6 us
    pallas_call x1, Pallas kernels, body(): pl.pallas_call(pack_kernel, out_shape=jax.ShapeDtypeStruct((PLANES, 8, ME...  2.27 us
    ppermute x1, starting transfers between devices, body(): sums = lax.ppermute(sums, ('cuts', 'slab'), routes())  2.01 us
    ppermute x1, starting transfers between devices, body(): got = lax.ppermute(send, 'slab', partners())  1.91 us
  transfers between devices with their start and end apart: 2, of which 2 were waited for; matrix products, arithmetic and copies ran while one was open for 0% of the time, Pallas kernels for 0%

profile of v2, /device:TPU:16, one launch (start us, length us, event | category | flops | bytes accessed | tf_op | source)
XLA Modules:
  0.0 87.9 jit_solution(17943961857237127765)
XLA Ops:
  0.6 2.3 %pack.1 = bf16[16,8,3456]{2,1,0:T(8,128)(2,1)} custom-call(bf16[6,2,9216]{2,1,0:T(2,128)(2,1)} %bitcast.10, s32[72,128]{1,0:T(8,128)} %bitcast.13, f32[72,128]{1,0:T(8,128)} %bitcast.12, f32[72,128]{1,0:T(8,128)} %bitcast.11, f32[32]{0:T(128)} %table_ref.1), custom_call_target="tpu_custom_call" | custom-call | tf_op jit(solution)/shard_map/pack/pallas_call | solution.py:300
  2.9 36.0 %all_to_all.10 = bf16[16,8,3456]{2,1,0:T(8,128)(2,1)} all-to-all(bf16[16,8,3456]{2,1,0:T(8,128)(2,1)} %pack.1), channel_id=1, replica_groups=mesh['cuts'=32,'slab'=16] {'slab'}, dimensions={0} | all-to-all | bytes 1769472 | tf_op jit(solution)/shard_map/all_to_all | solution.py:317
  38.9 7.6 %filter.1 = (f32[32,768]{1,0:T(8,128)}, f32[32,768]{1,0:T(8,128)}) custom-call(bf16[128,3456]{1,0:T(8,128)(2,1)} %bitcast.9, s32[32]{0:T(128)} %counts_ref.1, s32[192]{0:T(256)} %slice_ref.1, f32[192]{0:T(256)} %occupation_ref.1, f32[16,9]{1,0:T(8,128)} %coef_ref.1), custom_call_target="tpu_custom_call" | custom-call | tf_op jit(solution)/shard_map/filter/pallas_call | solution.py:264
  46.5 1.9 %collective-permute-start = (f32[32,768]{1,0:T(8,128)}, f32[32,768]{1,0:T(8,128)S(1)}, u32[]{:S(2)}, u32[]{:S(2)}) collective-permute-start(f32[32,768]{1,0:T(8,128)} %get-tuple-element.7), channel_id=1, source_target_pairs={{0,1},{1,0},{2,3},{3,2},{4,5},{5,4},{6,7},{7,6},{8,9},{9,8},{10,11... | collective-permute-start | bytes 294920 | tf_op jit(solution)/shard_map/ppermute | solution.py:319
  48.5 1.5 %collective-permute-done.got_ref = f32[32,768]{1,0:T(8,128)S(1)} collective-permute-done((f32[32,768]{1,0:T(8,128)}, f32[32,768]{1,0:T(8,128)S(1)}, u32[]{:S(2)}, u32[]{:S(2)}) %collective-permute-start) | collective-permute-done | bytes 98336 | tf_op jit(solution)/shard_map/ppermute | solution.py:319
  49.9 0.0 copy-start
  49.9 0.6 copy-done
  50.6 1.6 %join.1 = f32[32,1,768]{2,1,0:T(1,128)} custom-call(f32[32,768]{1,0:T(8,128)} %get-tuple-element.6.keep_ref, f32[32,768]{1,0:T(8,128)} %copy-done), custom_call_target="tpu_custom_call" | custom-call | tf_op jit(solution)/shard_map/join/pallas_call | solution.py:320
  52.2 21.4 %all_to_all.11.parts_ref = f32[32,1,768]{2,1,0:T(1,128)} all-to-all(f32[32,1,768]{2,1,0:T(1,128)} %join.1), channel_id=1, replica_groups=mesh['cuts'=32,'slab'=16] {'cuts'}, dimensions={0} | all-to-all | bytes 196608 | tf_op jit(solution)/shard_map/all_to_all | solution.py:327
  73.5 1.6 %total.1 = f32[2,288]{1,0:T(2,128)} custom-call(f32[32,1,768]{2,1,0:T(1,128)} %all_to_all.11.parts_ref), custom_call_target="tpu_custom_call" | custom-call | tf_op jit(solution)/shard_map/total/pallas_call | solution.py:328
  75.2 2.0 %collective-permute-start.1 = (f32[2,288]{1,0:T(2,128)}, f32[2,288]{1,0:T(2,128)S(1)}, u32[]{:S(2)}, u32[]{:S(2)}) collective-permute-start(f32[2,288]{1,0:T(2,128)} %total.1), channel_id=1, source_target_pairs={{0,0},{1,8},{2,64},{3,72},{4,128},{5,136},{6,192},{7,200},{8,256},... | collective-permute-start | bytes 6920 | tf_op jit(solution)/shard_map/ppermute | solution.py:335
  77.2 9.4 %collective-permute-done.1 = f32[2,288]{1,0:T(2,128)S(1)} collective-permute-done((f32[2,288]{1,0:T(2,128)}, f32[2,288]{1,0:T(2,128)S(1)}, u32[]{:S(2)}, u32[]{:S(2)}) %collective-permute-start.1) | collective-permute-done | bytes 2336 | tf_op jit(solution)/shard_map/ppermute | solution.py:335
  86.6 1.3 %multiply_subtract_fusion = (f32[1,288]{1,0:T(1,128)}, f32[1,288]{1,0:T(1,128)}, f32[1,288]{1,0:T(1,128)}, f32[1,288]{1,0:T(1,128)}) fusion(f32[1,9216]{1,0:T(1,128)} %param.17, s32[]{:T(128)S(6)} %select_n.4, f32[2,288]{1,0:T(2,128)S(1)} %collective-permute-done.1, f32[1,9216]{1,0:T(1,128)} %param.16), kind=kLoop, calls=%fused_computation.3 | loop fusion | flops 2304 | bytes 9220 | tf_op jit(solution)/shard_map/sub | solution.py:343
Async XLA Ops:
  46.5 3.4 %collective-permute-start = (f32[32,768]{1,0:T(8,128)}, f32[32,768]{1,0:T(8,128)S(1)}, u32[]{:S(2)}, u32[]{:S(2)}) collective-permute-start(f32[32,768]{1,0:T(8,128)} %get-tuple-element.7), channel_id=1, source_target_pairs={{0,1},{1,0},{2,3},{3,2},{4,5},{5,4},{6,7},{7,6},{8,9},{9,8},{10,11... | collective-permute-start | bytes 294920 | tf_op jit(solution)/shard_map/ppermute | solution.py:319
  49.9 0.6 copy-start
  75.2 11.4 %collective-permute-start.1 = (f32[2,288]{1,0:T(2,128)}, f32[2,288]{1,0:T(2,128)S(1)}, u32[]{:S(2)}, u32[]{:S(2)}) collective-permute-start(f32[2,288]{1,0:T(2,128)} %total.1), channel_id=1, source_target_pairs={{0,0},{1,8},{2,64},{3,72},{4,128},{5,136},{6,192},{7,200},{8,256},... | collective-permute-start | bytes 6920 | tf_op jit(solution)/shard_map/ppermute | solution.py:335

commit v3 on v2

--- a/solution.py
+++ b/solution.py
@@ -20,10 +20,13 @@
 WINDOWS = 8
 TILES = 72
 CORE = 9
-HALO = 6
-SPAN = CORE + 2 * HALO
-EXTRA = 6
-MESSAGE = SPAN + EXTRA
+QUAD = 4 * LANES
+MESSAGE = 3 * QUAD
+HALO = 2 * QUAD
+
+
+def slab_of(group, window):
+    return (window // 2) * 4 + group * 2 + window % 2
 
 
 def pack_kernel(quasi_ref, index_ref, mean_ref, pairing_ref, table_ref, out_ref, rows_ref, pot_ref):
@@ -45,42 +48,20 @@
             rows_ref[group, 3:4, lanes] = pot_ref[0, tile : tile + 1, :]
             rows_ref[group, 7:8, lanes] = pot_ref[1, tile : tile + 1, :]
     for window in range(WINDOWS):
-        first = CORE * window - HALO
-        begin, end = max(first, 0), min(first + SPAN, TILES)
-        for group in range(2):
-            slab = 2 * window + group
-            if begin > first:
-                out_ref[slab, :, : (begin - first) * LANES] = jnp.zeros(
-                    (8, (begin - first) * LANES), jnp.bfloat16
-                )
-            if end < first + SPAN:
-                out_ref[slab, :, (end - first) * LANES : SPAN * LANES] = jnp.zeros(
-                    (8, (first + SPAN - end) * LANES), jnp.bfloat16
-                )
-            out_ref[slab, :, (begin - first) * LANES : (end - first) * LANES] = rows_ref[
-                group, :, begin * LANES : end * LANES
-            ].astype(jnp.bfloat16)
-        for extra in range(EXTRA):
-            start = first + 4 * extra
-            pieces = []
-            low, top = max(start, 0), min(start + 4, TILES)
-            if low >= top:
-                values = jnp.zeros((4, LANES), jnp.float32)
-            else:
-                values = pairing_ref[low:top, :]
-                if low > start:
-                    values = jnp.concatenate(
-                        [jnp.zeros((low - start, LANES), jnp.float32), values], axis=0
-                    )
-                if top < start + 4:
-                    values = jnp.concatenate(
-                        [values, jnp.zeros((start + 4 - top, LANES), jnp.float32)], axis=0
-                    )
+        for quad in range(3):
+            first = CORE * window + 3 * quad
+            values = jnp.concatenate(
+                [pairing_ref[first : first + 3, :], jnp.zeros((1, LANES), jnp.float32)], axis=0
+            )
             upper = values.astype(jnp.bfloat16).astype(jnp.float32)
-            tile = jnp.concatenate([upper, values - upper], axis=0).astype(jnp.bfloat16)
-            lanes = slice((SPAN + extra) * LANES, (SPAN + extra + 1) * LANES)
-            out_ref[2 * window, :, lanes] = tile
-            out_ref[2 * window + 1, :, lanes] = tile
+            extra = jnp.concatenate([upper, values - upper], axis=0).astype(jnp.bfloat16)
+            start = quad * QUAD
+            for group in range(2):
+                slab = slab_of(group, window)
+                out_ref[slab, :, start : start + 3 * LANES] = rows_ref[
+                    group, :, first * LANES : (first + 3) * LANES
+                ].astype(jnp.bfloat16)
+                out_ref[slab, :, start + 3 * LANES : start + QUAD] = extra
 
 
 ROWS = 28
@@ -90,13 +71,13 @@
 
 
 def filter_kernel(
-    msg_ref, counts_ref, slice_ref, occupation_ref, coef_ref, keep_ref, send_ref,
+    low_ref, own_ref, high_ref, counts_ref, slice_ref, occupation_ref, coef_ref, out_ref,
     one_ref, two_ref, a_ref, c_ref, acc_ref, density_ref,
 ):
     cut = lax.axis_index("cuts")
     slab = lax.axis_index("slab")
-    group = slab % 2
-    window = slab // 2
+    group = (slab // 2) % 2
+    window = (slab // 4) * 2 + slab % 2
     scale = 2.0 / spectral_scale
     lane = lax.broadcasted_iota(jnp.int32, (8, LANES), 1)
     below_ok = jnp.where(window > 0, 1.0, 0.0)
@@ -119,7 +100,7 @@
         7 * PLANES,
         lambda i, row: (row == (i // 3) * 4 + i % 3) | ((i == 6) & (row % 4 == 3)),
     )
-    spread = chosen(4 * PLANES, lambda part, row: row % 4 == part)
+    spread = chosen(3 * PLANES, lambda part, row: row % 4 == part)
 
     for ref in (one_ref, two_ref):
         for block in range(6 * ROWS + 1):
@@ -138,16 +119,21 @@
         ]
         return [jnp.where(ok, row, 0.0) for row in rows]
 
-    fields = []
-    for extra in range(EXTRA):
-        lanes = slice((SPAN + extra) * LANES, (SPAN + extra + 1) * LANES)
-        part = jnp.dot(spread, msg_ref[:, lanes], preferred_element_type=jnp.float32)
-        fields += [part[16 * k : 16 * k + 16] for k in range(4)]
     for quad in range(ROWS // 4):
-        lanes = slice(3 * quad * LANES, 3 * (quad + 1) * LANES)
-        taken = jnp.dot(gather, msg_ref[:, lanes], preferred_element_type=jnp.float32)
+        if quad < 2:
+            ref, start = low_ref, quad * QUAD
+        elif quad < 5:
+            ref, start = own_ref, (quad - 2) * QUAD
+        else:
+            ref, start = high_ref, (quad - 5) * QUAD
+        taken = jnp.dot(
+            gather, ref[:, start : start + 3 * LANES], preferred_element_type=jnp.float32
+        )
+        part = jnp.dot(
+            spread, ref[:, start + 3 * LANES : start + QUAD], preferred_element_type=jnp.float32
+        )
         rows = unpack([taken[:, k * LANES : (k + 1) * LANES] for k in range(3)])
-        pairs = unpack(fields[3 * quad : 3 * quad + 3])
+        pairs = unpack([part[16 * k : 16 * k + 16] for k in range(3)])
         for k in range(4):
             y = 4 * quad + k
             mask = inside[place(y)]
@@ -223,19 +209,17 @@
 
     for density in range(2):
         for y in range(OWN):
-            quarter, row = y // 3, y % 3
-            lanes = slice((3 * density + row) * LANES, (3 * density + row + 1) * LANES)
+            lanes = slice((3 * density + y % 3) * LANES, (3 * density + y % 3 + 1) * LANES)
             at = (density * OWN + y) * 16
-            first, second = density_ref[at : at + 8, :], density_ref[at + 8 : at + 16, :]
-            mine = group == 0
-            keep_ref[8 * quarter : 8 * quarter + 8, lanes] = jnp.where(mine, first, second)
-            send_ref[8 * quarter : 8 * quarter + 8, lanes] = jnp.where(mine, second, first)
-
-
-def join_kernel(keep_ref, got_ref, out_ref):
-    total = keep_ref[...] + got_ref[...]
-    for piece in range(32):
-        out_ref[piece] = total[piece : piece + 1]
+            for high in range(2):
+                values = density_ref[at + 8 * high : at + 8 * high + 8, :]
+                for k in range(8):
+                    out_ref[piece_of(8 * high + k, y // 3), :, lanes] = values[k : k + 1]
+
+
+def piece_of(plane, quarter):
+    cut = 4 * (2 * (plane // 4) + plane % 2) + quarter
+    return 2 * cut + (plane // 2) % 2
 
 
 def sum_kernel(parts_ref, out_ref):
@@ -260,12 +244,13 @@
     return [pl.BlockSpec(memory_space=pltpu.SMEM)] * count
 
 
-def filter_call(message, counts, slot_slice, occupation, filter_coef):
+def filter_call(low, own, high, counts, slot_slice, occupation, filter_coef):
+    flat = [part.reshape(8 * PLANES, part.shape[2]) for part in (low, own, high)]
     return pl.pallas_call(
         filter_kernel,
-        out_shape=[jax.ShapeDtypeStruct((32, 6 * LANES), jnp.float32)] * 2,
-        in_specs=vmem(1) + smem(4),
-        out_specs=vmem(2),
+        out_shape=jax.ShapeDtypeStruct((64, 1, 6 * LANES), jnp.float32),
+        in_specs=vmem(3) + smem(4),
+        out_specs=pl.BlockSpec(memory_space=pltpu.VMEM),
         scratch_shapes=[
             pltpu.VMEM((6 * BLOCK + 8, LANES), jnp.float32),
             pltpu.VMEM((6 * BLOCK + 8, LANES), jnp.float32),
@@ -275,20 +260,33 @@
             pltpu.VMEM((2 * OWN * 16, LANES), jnp.float32),
         ],
         name="filter",
-    )(message.reshape(8 * PLANES, MESSAGE * LANES), counts, slot_slice, occupation, filter_coef)
-
-
-def partners():
-    return [(slab, slab ^ 1) for slab in range(16)]
+    )(*flat, counts, slot_slice, occupation, filter_coef)
+
+
+def neighbours(by):
+    return [
+        (slab_of(group, window), slab_of(group, window + by))
+        for group in range(2)
+        for window in range(WINDOWS)
+        if 0 <= window + by < WINDOWS
+    ]
+
+
+def summing_groups():
+    return [
+        [cut * 16 + slab_of(group, window) for cut in range(32) for group in range(2)]
+        for window in range(WINDOWS)
+    ]
 
 
 def routes():
     pairs = []
-    for cut in range(32):
-        for slab in range(16):
-            group, window = slab % 2, slab // 2
-            target = (4 * window + cut // 8) * 16 + 8 * group + cut % 8
-            pairs.append((cut * 16 + slab, target))
+    for window in range(WINDOWS):
+        for plane in range(PLANES):
+            for quarter in range(4):
+                piece = piece_of(plane, quarter)
+                source = (piece // 2) * 16 + slab_of(piece % 2, window)
+                pairs.append((source, (4 * window + quarter) * 16 + plane))
     return pairs
 
 
@@ -299,7 +297,7 @@
     packed = jnp.transpose(quasi, (1, 2, 0, 3)).reshape(CAP, 2, TILES * LANES)
     message = pl.pallas_call(
         pack_kernel,
-        out_shape=jax.ShapeDtypeStruct((PLANES, 8, MESSAGE * LANES), jnp.bfloat16),
+        out_shape=jax.ShapeDtypeStruct((PLANES, 8, MESSAGE), jnp.bfloat16),
         in_specs=vmem(4) + smem(1),
         out_specs=pl.BlockSpec(memory_space=pltpu.VMEM),
         scratch_shapes=[
@@ -315,16 +313,12 @@
         trap_table,
     )
     message = lax.all_to_all(message, "slab", 0, 0, tiled=True)
-    keep, send = filter_call(message, counts, slot_slice, occupation, filter_coef)
-    got = lax.ppermute(send, "slab", partners())
-    parts = pl.pallas_call(
-        join_kernel,
-        out_shape=jax.ShapeDtypeStruct((32, 1, 6 * LANES), jnp.float32),
-        in_specs=vmem(2),
-        out_specs=pl.BlockSpec(memory_space=pltpu.VMEM),
-        name="join",
-    )(keep, got)
-    parts = lax.all_to_all(parts, "cuts", 0, 0, tiled=True)
+    low = lax.ppermute(message[:, :, MESSAGE - HALO :], "slab", neighbours(1))
+    high = lax.ppermute(message[:, :, :HALO], "slab", neighbours(-1))
+    parts = filter_call(low, message, high, counts, slot_slice, occupation, filter_coef)
+    parts = lax.all_to_all(
+        parts, ("cuts", "slab"), 0, 0, axis_index_groups=summing_groups(), tiled=True
+    )
     sums = pl.pallas_call(
         sum_kernel,
         out_shape=jax.ShapeDtypeStruct((2, 288), jnp.float32),

time: 88.3 us -> 87.7 us (level)
  the two profiles are of different devices: /device:TPU:16 before, /device:TPU:4 now
where the time goes in v3:
time: 87.7 us; the launch traced here: 87.2 us
  blocking collectives  50.5 us (58%)
  waiting for transfers between devices  15.6 us (18%)
  Pallas kernels  11.4 us (13%)
  starting transfers between devices  6.22 us (7%)
  local copies, waits for them, and re-layouts  1.44 us (2%)
  other arithmetic  1.34 us (2%)
    all_to_all x1, blocking collectives, body(): lax.all_to_all(parts, ('cuts', 'slab'), 0, 0, axis_index_groups=summing_g...  27.8 us
    all_to_all x1, blocking collectives, body(): message = lax.all_to_all(message, 'slab', 0, 0, tiled=True)  22.7 us
    ppermute x1, waiting for transfers between devices, body(): sums = lax.ppermute(sums, ('cuts', 'slab'), routes())  10.1 us
    pallas_call x1, Pallas kernels, filter_call(): pl.pallas_call(filter_kernel, out_shape=jax.ShapeDtypeStruct((64, 1, 6 *...  7.7 us
    ppermute x1, waiting for transfers between devices, body(): low = lax.ppermute(message[:, :, MESSAGE - HALO:], 'slab', neighbours(1))  3.82 us
    ppermute x1, starting transfers between devices, body(): high = lax.ppermute(message[:, :, :HALO], 'slab', neighbours(-1))  2.2 us
    ppermute x1, starting transfers between devices, body(): low = lax.ppermute(message[:, :, MESSAGE - HALO:], 'slab', neighbours(1))  2.11 us
    pallas_call x1, Pallas kernels, body(): pl.pallas_call(pack_kernel, out_shape=jax.ShapeDtypeStruct((PLANES, 8, ME...  2.02 us
  transfers between devices with their start and end apart: 3, of which 3 were waited for; matrix products, arithmetic and copies ran while one was open for 0% of the time, Pallas kernels for 0%

profile of v3, /device:TPU:4, one launch (start us, length us, event | category | flops | bytes accessed | tf_op | source)
XLA Modules:
  0.0 87.2 jit_solution(17257577329639345769)
XLA Ops:
  0.6 2.0 %pack.1 = bf16[16,8,1536]{2,1,0:T(8,128)(2,1)} custom-call(bf16[6,2,9216]{2,1,0:T(2,128)(2,1)} %bitcast.14, s32[72,128]{1,0:T(8,128)} %bitcast.17, f32[72,128]{1,0:T(8,128)} %bitcast.16, f32[72,128]{1,0:T(8,128)} %bitcast.15, f32[32]{0:T(128)} %table_ref.1), custom_call_target="tpu_custom_call" | custom-call | tf_op jit(solution)/shard_map/pack/pallas_call | solution.py:298
  2.6 22.7 %all_to_all.10 = bf16[16,8,1536]{2,1,0:T(8,128)(2,1)S(1)} all-to-all(bf16[16,8,1536]{2,1,0:T(8,128)(2,1)} %pack.1), channel_id=1, replica_groups=mesh['cuts'=32,'slab'=16] {'slab'}, dimensions={0} | all-to-all | bytes 786432 | tf_op jit(solution)/shard_map/all_to_all | solution.py:315
  25.4 0.0 copy-start
  25.4 0.7 copy-done
  26.1 2.2 %collective-permute-start.1 = (bf16[16,8,1024]{2,1,0:T(8,128)(2,1)S(1)}, bf16[16,8,1024]{2,1,0:T(8,128)(2,1)S(1)}, u32[]{:S(2)}, u32[]{:S(2)}) collective-permute-start(bf16[16,8,1024]{2,1,0:T(8,128)(2,1)S(1)} %get-tuple-element.8), channel_id=1, source_target_pairs={{1,0},{4,1},{5,4},{8,5},{9,8},{12,9},{13,12},{3,2},{6,3},{7,6},{10... | collective-permute-start | bytes 786440 | tf_op jit(solution)/shard_map/ppermute | solution.py:317
  28.3 2.1 %collective-permute-start = (bf16[16,8,1024]{2,1,0:T(8,128)(2,1)S(1)}, bf16[16,8,1024]{2,1,0:T(8,128)(2,1)S(1)}, u32[]{:S(2)}, u32[]{:S(2)}) collective-permute-start(bf16[16,8,1024]{2,1,0:T(8,128)(2,1)S(1)} %get-tuple-element.9), channel_id=1, source_target_pairs={{0,1},{1,4},{4,5},{5,8},{8,9},{9,12},{12,13},{2,3},{3,6},{6,7},{7,... | collective-permute-start | bytes 786440 | tf_op jit(solution)/shard_map/ppermute | solution.py:316
  30.5 1.8 %collective-permute-done.1 = bf16[16,8,1024]{2,1,0:T(8,128)(2,1)S(1)} collective-permute-done((bf16[16,8,1024]{2,1,0:T(8,128)(2,1)S(1)}, bf16[16,8,1024]{2,1,0:T(8,128)(2,1)S(1)}, u32[]{:S(2)}, u32[]{:S(2)}) %collective-permute-start.1) | collective-permute-done | bytes 262176 | tf_op jit(solution)/shard_map/ppermute | solution.py:317
  32.2 0.0 copy-start.1
  32.2 3.8 %collective-permute-done = bf16[16,8,1024]{2,1,0:T(8,128)(2,1)S(1)} collective-permute-done((bf16[16,8,1024]{2,1,0:T(8,128)(2,1)S(1)}, bf16[16,8,1024]{2,1,0:T(8,128)(2,1)S(1)}, u32[]{:S(2)}, u32[]{:S(2)}) %collective-permute-start) | collective-permute-done | bytes 262176 | tf_op jit(solution)/shard_map/ppermute | solution.py:316
  36.0 0.0 copy-start.2
  36.0 0.0 copy-done.1
  36.0 0.7 copy-done.2
  36.7 7.7 %filter.1 = f32[64,1,768]{2,1,0:T(1,128)} custom-call(bf16[128,1024]{1,0:T(8,128)(2,1)} %bitcast.13, bf16[128,1536]{1,0:T(8,128)(2,1)} %bitcast.11, bf16[128,1024]{1,0:T(8,128)(2,1)} %bitcast.12, s32[32]{0:T(128)} %counts_ref.1, s32[192]{0:T(256)} %slice_ref.1, f32[192]{0:T(256)} %occupation_ref.1, f32[16,9]{1,0:T(8,128)} %coef_ref.1), custom_call_target="tpu_custom_call" | custom-call | tf_op jit(solution)/shard_map/filter/pallas_call | solution.py:249
  44.4 27.8 %all_to_all.11.parts_ref = f32[64,1,768]{2,1,0:T(1,128)} all-to-all(f32[64,1,768]{2,1,0:T(1,128)} %filter.1), channel_id=1, replica_groups={{0,2,16,18,32,34,48,50,64,66,80,82,96,98,112,114,128,130,144,146,160,16..., dimensions={0} | all-to-all | bytes 393216 | tf_op jit(solution)/shard_map/all_to_all | solution.py:319
  72.2 1.7 %total.1 = f32[2,288]{1,0:T(2,128)} custom-call(f32[64,1,768]{2,1,0:T(1,128)} %all_to_all.11.parts_ref), custom_call_target="tpu_custom_call" | custom-call | tf_op jit(solution)/shard_map/total/pallas_call | solution.py:322
  73.9 1.9 %collective-permute-start.2 = (f32[2,288]{1,0:T(2,128)}, f32[2,288]{1,0:T(2,128)S(1)}, u32[]{:S(2)}, u32[]{:S(2)}) collective-permute-start(f32[2,288]{1,0:T(2,128)} %total.1), channel_id=1, source_target_pairs={{0,0},{16,16},{32,32},{48,48},{64,1},{80,17},{96,33},{112,49},{2,2... | collective-permute-start | bytes 6920 | tf_op jit(solution)/shard_map/ppermute | solution.py:329
  75.8 10.1 %collective-permute-done.2 = f32[2,288]{1,0:T(2,128)S(1)} collective-permute-done((f32[2,288]{1,0:T(2,128)}, f32[2,288]{1,0:T(2,128)S(1)}, u32[]{:S(2)}, u32[]{:S(2)}) %collective-permute-start.2) | collective-permute-done | bytes 2336 | tf_op jit(solution)/shard_map/ppermute | solution.py:329
  85.9 1.3 %multiply_subtract_fusion = (f32[1,288]{1,0:T(1,128)}, f32[1,288]{1,0:T(1,128)}, f32[1,288]{1,0:T(1,128)}, f32[1,288]{1,0:T(1,128)}) fusion(f32[1,9216]{1,0:T(1,128)} %param.17, s32[]{:T(128)S(6)} %select_n.4, f32[2,288]{1,0:T(2,128)S(1)} %collective-permute-done.2, f32[1,9216]{1,0:T(1,128)} %param.16), kind=kLoop, calls=%fused_computation.3 | loop fusion | flops 2304 | bytes 9220 | tf_op jit(solution)/shard_map/sub | solution.py:337
  (1 shorter events, 0.0 us)
Async XLA Ops:
  25.4 0.7 copy-start
  26.1 6.1 %collective-permute-start.1 = (bf16[16,8,1024]{2,1,0:T(8,128)(2,1)S(1)}, bf16[16,8,1024]{2,1,0:T(8,128)(2,1)S(1)}, u32[]{:S(2)}, u32[]{:S(2)}) collective-permute-start(bf16[16,8,1024]{2,1,0:T(8,128)(2,1)S(1)} %get-tuple-element.8), channel_id=1, source_target_pairs={{1,0},{4,1},{5,4},{8,5},{9,8},{12,9},{13,12},{3,2},{6,3},{7,6},{10... | collective-permute-start | bytes 786440 | tf_op jit(solution)/shard_map/ppermute | solution.py:317
  28.3 7.7 %collective-permute-start = (bf16[16,8,1024]{2,1,0:T(8,128)(2,1)S(1)}, bf16[16,8,1024]{2,1,0:T(8,128)(2,1)S(1)}, u32[]{:S(2)}, u32[]{:S(2)}) collective-permute-start(bf16[16,8,1024]{2,1,0:T(8,128)(2,1)S(1)} %get-tuple-element.9), channel_id=1, source_target_pairs={{0,1},{1,4},{4,5},{5,8},{8,9},{9,12},{12,13},{2,3},{3,6},{6,7},{7,... | collective-permute-start | bytes 786440 | tf_op jit(solution)/shard_map/ppermute | solution.py:316
  32.2 3.8 %copy-start.1 = (bf16[16,8,1024]{2,1,0:T(8,128)(2,1)}, bf16[16,8,1024]{2,1,0:T(8,128)(2,1)S(1)}, u32[]{:S(2)}) copy-start(bf16[16,8,1024]{2,1,0:T(8,128)(2,1)S(1)} %collective-permute-done.1) | copy-start | bytes 786436
  36.0 0.7 copy-start.2
  73.9 12.0 %collective-permute-start.2 = (f32[2,288]{1,0:T(2,128)}, f32[2,288]{1,0:T(2,128)S(1)}, u32[]{:S(2)}, u32[]{:S(2)}) collective-permute-start(f32[2,288]{1,0:T(2,128)} %total.1), channel_id=1, source_target_pairs={{0,0},{16,16},{32,32},{48,48},{64,1},{80,17},{96,33},{112,49},{2,2... | collective-permute-start | bytes 6920 | tf_op jit(solution)/shard_map/ppermute | solution.py:329

commit v4 on v3

--- a/solution.py
+++ b/solution.py
@@ -21,15 +21,18 @@
 TILES = 72
 CORE = 9
 QUAD = 4 * LANES
-MESSAGE = 3 * QUAD
-HALO = 2 * QUAD
+QUADS = 24
+SPAN = 7
 
 
 def slab_of(group, window):
     return (window // 2) * 4 + group * 2 + window % 2
 
 
-def pack_kernel(quasi_ref, index_ref, mean_ref, pairing_ref, table_ref, out_ref, rows_ref, pot_ref):
+def pack_kernel(
+    quasi_ref, index_ref, mean_ref, pairing_ref, table_ref, mine_ref, theirs_ref, rows_ref, pot_ref
+):
+    half = (lax.axis_index("slab") // 2) % 2
     index = index_ref[...]
     looked = jnp.zeros(index.shape, jnp.float32)
     for level in range(table_ref.shape[0]):
@@ -38,30 +41,48 @@
     high = potential.astype(jnp.bfloat16).astype(jnp.float32)
     pot_ref[0] = high
     pot_ref[1] = potential - high
-    for group in range(2):
+    for side, group in ((0, half), (1, 1 - half)):
         for slot in range(3):
             pair = quasi_ref[3 * group + slot].astype(jnp.float32)
-            rows_ref[group, slot : slot + 1, :] = pair[0:1]
-            rows_ref[group, 4 + slot : 5 + slot, :] = pair[1:2]
+            rows_ref[side, slot : slot + 1, :] = pair[0:1]
+            rows_ref[side, 4 + slot : 5 + slot, :] = pair[1:2]
         for tile in range(TILES):
             lanes = slice(tile * LANES, (tile + 1) * LANES)
-            rows_ref[group, 3:4, lanes] = pot_ref[0, tile : tile + 1, :]
-            rows_ref[group, 7:8, lanes] = pot_ref[1, tile : tile + 1, :]
+            rows_ref[side, 3:4, lanes] = pot_ref[0, tile : tile + 1, :]
+            rows_ref[side, 7:8, lanes] = pot_ref[1, tile : tile + 1, :]
+    for quad in range(QUADS):
+        first = 3 * quad
+        values = jnp.concatenate(
+            [pairing_ref[first : first + 3, :], jnp.zeros((1, LANES), jnp.float32)], axis=0
+        )
+        upper = values.astype(jnp.bfloat16).astype(jnp.float32)
+        extra = jnp.concatenate([upper, values - upper], axis=0).astype(jnp.bfloat16)
+        start = quad * QUAD
+        for side, out_ref in ((0, mine_ref), (1, theirs_ref)):
+            out_ref[:, start : start + 3 * LANES] = rows_ref[
+                side, :, first * LANES : (first + 3) * LANES
+            ].astype(jnp.bfloat16)
+            out_ref[:, start + 3 * LANES : start + QUAD] = extra
+
+
+def window_kernel(mine_ref, got_ref, out_ref):
+    half = (lax.axis_index("slab") // 2) % 2
     for window in range(WINDOWS):
-        for quad in range(3):
-            first = CORE * window + 3 * quad
-            values = jnp.concatenate(
-                [pairing_ref[first : first + 3, :], jnp.zeros((1, LANES), jnp.float32)], axis=0
-            )
-            upper = values.astype(jnp.bfloat16).astype(jnp.float32)
-            extra = jnp.concatenate([upper, values - upper], axis=0).astype(jnp.bfloat16)
-            start = quad * QUAD
-            for group in range(2):
-                slab = slab_of(group, window)
-                out_ref[slab, :, start : start + 3 * LANES] = rows_ref[
-                    group, :, first * LANES : (first + 3) * LANES
-                ].astype(jnp.bfloat16)
-                out_ref[slab, :, start + 3 * LANES : start + QUAD] = extra
+        first = 3 * window - 2
+        begin, end = max(first, 0), min(first + SPAN, QUADS)
+        before, after = begin - first, first + SPAN - end
+        for ref, place in ((mine_ref, half), (got_ref, 1 - half)):
+            if before:
+                out_ref[window, place, :, : before * QUAD] = jnp.zeros(
+                    (8, before * QUAD), jnp.bfloat16
+                )
+            if after:
+                out_ref[window, place, :, (SPAN - after) * QUAD :] = jnp.zeros(
+                    (8, after * QUAD), jnp.bfloat16
+                )
+            out_ref[window, place, :, before * QUAD : (SPAN - after) * QUAD] = ref[
+                :, begin * QUAD : end * QUAD
+            ]
 
 
 ROWS = 28
@@ -71,7 +92,7 @@
 
 
 def filter_kernel(
-    low_ref, own_ref, high_ref, counts_ref, slice_ref, occupation_ref, coef_ref, out_ref,
+    msg_ref, counts_ref, slice_ref, occupation_ref, coef_ref, out_ref,
     one_ref, two_ref, a_ref, c_ref, acc_ref, density_ref,
 ):
     cut = lax.axis_index("cuts")
@@ -93,7 +114,8 @@
     def chosen(count, pick):
         out = lax.broadcasted_iota(jnp.int32, (count, LANES), 0)
         source = lax.broadcasted_iota(jnp.int32, (count, LANES), 1)
-        same = (out % PLANES) == (source // 8)
+        chip, core, half = source // 32, (source // 16) % 2, (source // 8) % 2
+        same = (out % PLANES) == 4 * chip + 2 * half + core
         return jnp.where(same & pick(out // PLANES, source % 8), 1.0, 0.0).astype(jnp.bfloat16)
 
     gather = chosen(
@@ -120,17 +142,12 @@
         return [jnp.where(ok, row, 0.0) for row in rows]
 
     for quad in range(ROWS // 4):
-        if quad < 2:
-            ref, start = low_ref, quad * QUAD
-        elif quad < 5:
-            ref, start = own_ref, (quad - 2) * QUAD
-        else:
-            ref, start = high_ref, (quad - 5) * QUAD
+        start = quad * QUAD
         taken = jnp.dot(
-            gather, ref[:, start : start + 3 * LANES], preferred_element_type=jnp.float32
+            gather, msg_ref[:, start : start + 3 * LANES], preferred_element_type=jnp.float32
         )
         part = jnp.dot(
-            spread, ref[:, start + 3 * LANES : start + QUAD], preferred_element_type=jnp.float32
+            spread, msg_ref[:, start + 3 * LANES : start + QUAD], preferred_element_type=jnp.float32
         )
         rows = unpack([taken[:, k * LANES : (k + 1) * LANES] for k in range(3)])
         pairs = unpack([part[16 * k : 16 * k + 16] for k in range(3)])
@@ -207,14 +224,26 @@
 
     lax.fori_loop(0, 3, vector, 0)
 
-    for density in range(2):
-        for y in range(OWN):
-            lanes = slice((3 * density + y % 3) * LANES, (3 * density + y % 3 + 1) * LANES)
-            at = (density * OWN + y) * 16
-            for high in range(2):
-                values = density_ref[at + 8 * high : at + 8 * high + 8, :]
-                for k in range(8):
-                    out_ref[piece_of(8 * high + k, y // 3), :, lanes] = values[k : k + 1]
+    for quarter in range(4):
+        for high in range(2):
+            at = 48 * quarter + 8 * high
+            normal = [density_ref[at + 16 * k : at + 16 * k + 8, :] for k in range(3)]
+            at = at + OWN * 16
+            other = [density_ref[at + 16 * k : at + 16 * k + 8, :] for k in range(3)]
+            second, third = pltpu.roll(normal[1], 96, 1), pltpu.roll(normal[2], 64, 1)
+            last = pltpu.roll(other[2], 96, 1)
+            tiles = [
+                jnp.where(lane < 96, normal[0], second),
+                jnp.where(lane < 64, second, third),
+                jnp.where(lane < 32, third, pltpu.roll(other[0], 32, 1)),
+                jnp.where(lane < 96, other[1], last),
+                last[:, :64],
+            ]
+            for k in range(8):
+                piece = piece_of(8 * high + k, quarter)
+                for tile, values in enumerate(tiles):
+                    lanes = slice(tile * LANES, tile * LANES + values.shape[1])
+                    out_ref[piece, :, lanes] = values[k : k + 1]
 
 
 def piece_of(plane, quarter):
@@ -223,17 +252,7 @@
 
 
 def sum_kernel(parts_ref, out_ref):
-    total = jnp.sum(parts_ref[...], axis=0)
-    lane = lax.broadcasted_iota(jnp.int32, (1, LANES), 1)
-    for density in range(2):
-        first, second, third = [
-            total[:, (3 * density + k) * LANES : (3 * density + k + 1) * LANES] for k in range(3)
-        ]
-        second, third = pltpu.roll(second, 96, 1), pltpu.roll(third, 64, 1)
-        row = slice(density, density + 1)
-        out_ref[row, 0:128] = jnp.where(lane < 96, first, second)
-        out_ref[row, 128:256] = jnp.where(lane < 64, second, third)
-        out_ref[row, 256:288] = third[:, :32]
+    out_ref[...] = jnp.sum(parts_ref[...], axis=0)
 
 
 def vmem(count):
@@ -244,12 +263,15 @@
     return [pl.BlockSpec(memory_space=pltpu.SMEM)] * count
 
 
-def filter_call(low, own, high, counts, slot_slice, occupation, filter_coef):
-    flat = [part.reshape(8 * PLANES, part.shape[2]) for part in (low, own, high)]
+def grant(mebibytes):
+    return pltpu.CompilerParams(vmem_limit_bytes=mebibytes << 20)
+
+
+def filter_call(message, counts, slot_slice, occupation, filter_coef):
     return pl.pallas_call(
         filter_kernel,
-        out_shape=jax.ShapeDtypeStruct((64, 1, 6 * LANES), jnp.float32),
-        in_specs=vmem(3) + smem(4),
+        out_shape=jax.ShapeDtypeStruct((64, 1, 2 * 288), jnp.float32),
+        in_specs=vmem(1) + smem(4),
         out_specs=pl.BlockSpec(memory_space=pltpu.VMEM),
         scratch_shapes=[
             pltpu.VMEM((6 * BLOCK + 8, LANES), jnp.float32),
@@ -259,17 +281,13 @@
             pltpu.VMEM((2 * OWN * 16, LANES), jnp.float32),
             pltpu.VMEM((2 * OWN * 16, LANES), jnp.float32),
         ],
+        compiler_params=grant(16),
         name="filter",
-    )(*flat, counts, slot_slice, occupation, filter_coef)
-
-
-def neighbours(by):
-    return [
-        (slab_of(group, window), slab_of(group, window + by))
-        for group in range(2)
-        for window in range(WINDOWS)
-        if 0 <= window + by < WINDOWS
-    ]
+    )(message.reshape(8 * PLANES, SPAN * QUAD), counts, slot_slice, occupation, filter_coef)
+
+
+def window_groups():
+    return [[slab_of(group, window) for window in range(WINDOWS)] for group in range(2)]
 
 
 def summing_groups():
@@ -295,15 +313,16 @@
 ):
     share = mean_field.shape[1] // lax.axis_size("cuts")
     packed = jnp.transpose(quasi, (1, 2, 0, 3)).reshape(CAP, 2, TILES * LANES)
-    message = pl.pallas_call(
+    mine, theirs = pl.pallas_call(
         pack_kernel,
-        out_shape=jax.ShapeDtypeStruct((PLANES, 8, MESSAGE), jnp.bfloat16),
+        out_shape=[jax.ShapeDtypeStruct((8, QUADS * QUAD), jnp.bfloat16)] * 2,
         in_specs=vmem(4) + smem(1),
-        out_specs=pl.BlockSpec(memory_space=pltpu.VMEM),
+        out_specs=vmem(2),
         scratch_shapes=[
             pltpu.VMEM((2, 8, TILES * LANES), jnp.float32),
             pltpu.VMEM((2, TILES, LANES), jnp.float32),
         ],
+        compiler_params=grant(8),
         name="pack",
     )(
         packed,
@@ -312,26 +331,36 @@
         pairing.reshape(TILES, LANES),
         trap_table,
     )
-    message = lax.all_to_all(message, "slab", 0, 0, tiled=True)
-    low = lax.ppermute(message[:, :, MESSAGE - HALO :], "slab", neighbours(1))
-    high = lax.ppermute(message[:, :, :HALO], "slab", neighbours(-1))
-    parts = filter_call(low, message, high, counts, slot_slice, occupation, filter_coef)
+    got = lax.ppermute(theirs, "slab", [(slab, slab ^ 2) for slab in range(16)])
+    message = pl.pallas_call(
+        window_kernel,
+        out_shape=jax.ShapeDtypeStruct((WINDOWS, 2, 8, SPAN * QUAD), jnp.bfloat16),
+        in_specs=vmem(2),
+        out_specs=pl.BlockSpec(memory_space=pltpu.VMEM),
+        compiler_params=grant(8),
+        name="window",
+    )(mine, got)
+    message = lax.all_to_all(
+        message, "slab", 0, 0, axis_index_groups=window_groups(), tiled=True
+    )
+    parts = filter_call(message, counts, slot_slice, occupation, filter_coef)
     parts = lax.all_to_all(
         parts, ("cuts", "slab"), 0, 0, axis_index_groups=summing_groups(), tiled=True
     )
     sums = pl.pallas_call(
         sum_kernel,
-        out_shape=jax.ShapeDtypeStruct((2, 288), jnp.float32),
+        out_shape=jax.ShapeDtypeStruct((1, 2 * 288), jnp.float32),
         in_specs=vmem(1),
         out_specs=pl.BlockSpec(memory_space=pltpu.VMEM),
+        compiler_params=grant(4),
         name="total",
     )(parts)
     sums = lax.ppermute(sums, ("cuts", "slab"), routes())
     offset = lax.axis_index("cuts") * share
     mean_local = lax.dynamic_slice_in_dim(mean_field, offset, share, 1)
     pairing_local = lax.dynamic_slice_in_dim(pairing, offset, share, 1)
-    normal_density = sums[0:1]
-    anomalous_density = sums[1:2]
+    normal_density = sums[:, :share]
+    anomalous_density = sums[:, share:]
     cube_root = jnp.cbrt(normal_density + density_floor)
     new_mean_field = 0.5 * mean_local + 0.5 * (beta_coef * cube_root * cube_root - chem_level)
     new_pairing = 0.5 * pairing_local - coupling * anomalous_density

time: 87.7 us -> 89.6 us (1.022)
  starting transfers between devices: 6.22 us -> 12.1 us
  Pallas kernels: 11.4 us -> 7.63 us
  local copies, waits for them, and re-layouts: 1.44 us -> 4.57 us
  blocking collectives: 50.5 us -> 48.7 us
  waiting for transfers between devices: 15.6 us -> 14.1 us
    pallas_call x3 -> x4, Pallas kernels: 11.4 us -> 7.63 us  [the longest x1 6.6 us: filter_call(): pl.pallas_call(filter_kernel, out_shape=jax.ShapeDtypeStruct((64, 1, 2 *...]
    ppermute x2 -> x1, starting transfers between devices: 4.31 us -> 7.73 us  [body(): got = lax.ppermute(theirs, 'slab', [(slab, slab ^ 2) for slab in range(16)])]
    unnamed x6 -> x18, local copies, waits for them, and re-layouts: 1.4 us -> 4.57 us
    all_to_all x1, blocking collectives: 22.7 us -> 19.7 us  [body(): lax.all_to_all(message, 'slab', 0, 0, axis_index_groups=window_groups(),...]
    ppermute x1, waiting for transfers between devices: 10.1 us -> 7.4 us  [body(): sums = lax.ppermute(sums, ('cuts', 'slab'), routes())]
    ppermute x1, starting transfers between devices: 1.91 us -> 4.38 us  [body(): sums = lax.ppermute(sums, ('cuts', 'slab'), routes())]
    all_to_all x1, blocking collectives: 27.8 us -> 28.9 us  [body(): lax.all_to_all(parts, ('cuts', 'slab'), 0, 0, axis_index_groups=summing_g...]
    ppermute x2 -> x1, waiting for transfers between devices: 5.57 us -> 6.7 us  [body(): got = lax.ppermute(theirs, 'slab', [(slab, slab ^ 2) for slab in range(16)])]
  transfers between devices with their start and end apart: 3 -> 2, of which waited for: 3 -> 2; matrix products, arithmetic and copies ran while one was open for 0% -> 0% of each run, Pallas kernels for 0% -> 0%
where the time goes in v4:
time: 89.6 us; the launch traced here: 89.1 us
  blocking collectives  48.7 us (54%)
  waiting for transfers between devices  14.1 us (16%)
  starting transfers between devices  12.1 us (14%)
  Pallas kernels  7.63 us (9%)
  local copies, waits for them, and re-layouts  4.57 us (5%)
  other arithmetic  1.35 us (2%)
    all_to_all x1, blocking collectives, body(): lax.all_to_all(parts, ('cuts', 'slab'), 0, 0, axis_index_groups=summing_g...  28.9 us
    all_to_all x1, blocking collectives, body(): lax.all_to_all(message, 'slab', 0, 0, axis_index_groups=window_groups(),...  19.7 us
    ppermute x1, starting transfers between devices, body(): got = lax.ppermute(theirs, 'slab', [(slab, slab ^ 2) for slab in range(16)])  7.73 us
    ppermute x1, waiting for transfers between devices, body(): sums = lax.ppermute(sums, ('cuts', 'slab'), routes())  7.4 us
    ppermute x1, waiting for transfers between devices, body(): got = lax.ppermute(theirs, 'slab', [(slab, slab ^ 2) for slab in range(16)])  6.7 us
    pallas_call x1, Pallas kernels, filter_call(): pl.pallas_call(filter_kernel, out_shape=jax.ShapeDtypeStruct((64, 1, 2 *...  6.6 us
    unnamed x18, local copies, waits for them, and re-layouts  4.57 us
    ppermute x1, starting transfers between devices, body(): sums = lax.ppermute(sums, ('cuts', 'slab'), routes())  4.38 us
  transfers between devices with their start and end apart: 2, of which 2 were waited for; matrix products, arithmetic and copies ran while one was open for 0% of the time, Pallas kernels for 0%

profile of v4, /device:TPU:4, one launch (start us, length us, event | category | flops | bytes accessed | tf_op | source)
XLA Modules:
  0.0 89.1 jit_solution(18238007365079247980)
XLA Ops:
  0.6 0.0 copy-start.7
  0.6 0.6 copy-done.7
  1.3 0.0 copy-start
  1.3 0.9 %copy-done = bf16[2,6,1,9216]{3,0,2,1:T(2,128)(2,1)S(1)} copy-done((bf16[2,6,1,9216]{3,0,2,1:T(2,128)(2,1)S(1)}, bf16[2,6,1,9216]{3,0,2,1:T(2,128)(2,1)}, u32[]{:S(2)}) %copy-start) | copy-done | bytes 221208
  2.2 0.8 copy-done.1
  3.0 0.8 copy-done.2
  3.8 0.8 copy-done.3
  4.5 0.8 pack.1
  5.4 7.7 %collective-permute-start = (bf16[8,12288]{1,0:T(8,128)(2,1)S(1)}, bf16[8,12288]{1,0:T(8,128)(2,1)S(1)}, u32[]{:S(2)}, u32[]{:S(2)}) collective-permute-start(bf16[8,12288]{1,0:T(8,128)(2,1)S(1)} %get-tuple-element.7), channel_id=1, source_target_pairs={{0,2},{1,3},{2,0},{3,1},{4,6},{5,7},{6,4},{7,5},{8,10},{9,11},{10,... | collective-permute-start | bytes 589832 | tf_op jit(solution)/shard_map/ppermute | solution.py:334
  13.1 6.7 %collective-permute-done.got_ref = bf16[8,12288]{1,0:T(8,128)(2,1)S(1)} collective-permute-done((bf16[8,12288]{1,0:T(8,128)(2,1)S(1)}, bf16[8,12288]{1,0:T(8,128)(2,1)S(1)}, u32[]{:S(2)}, u32[]{:S(2)}) %collective-permute-start) | collective-permute-done | bytes 196640 | tf_op jit(solution)/shard_map/ppermute | solution.py:334
  19.8 0.1 window.1
  19.9 0.0 copy-start.4
  19.9 0.0 copy-start.6
  19.9 19.7 %all_to_all.10 = bf16[8,2,8,3584]{3,2,1,0:T(8,128)(2,1)S(1)} all-to-all(bf16[8,2,8,3584]{3,2,1,0:T(8,128)(2,1)S(1)} %window.1), channel_id=1, replica_groups={{0,1,4,5,8,9,12,13},{2,3,6,7,10,11,14,15},{16,17,20,21,24,25,28,29},{18..., dimensions={0} | all-to-all | bytes 1835008 | tf_op jit(solution)/shard_map/all_to_all | solution.py:343
  39.6 0.0 copy-done.4
  39.7 0.0 copy-done.6
  39.7 0.7 copy-done.5
  40.3 0.0 copy-done.8
  40.3 6.6 %filter.1 = f32[64,1,576]{2,1,0:T(1,128)S(1)} custom-call(bf16[128,3584]{1,0:T(8,128)(2,1)S(1)} %bitcast.9, s32[32]{0:T(128)S(1)} %copy-done.8, s32[192]{0:T(256)S(1)} %copy-done.5, f32[192]{0:T(256)S(1)} %copy-done.6, f32[16,9]{1,0:T(8,128)S(1)} %copy-done.4), custom_call_target="tpu_custom_call" | custom-call | tf_op jit(solution)/shard_map/filter/pallas_call | solution.py:271
  46.9 28.9 %all_to_all.11.parts_ref = f32[64,1,576]{2,1,0:T(1,128)S(1)} all-to-all(f32[64,1,576]{2,1,0:T(1,128)S(1)} %filter.1), channel_id=1, replica_groups={{0,2,16,18,32,34,48,50,64,66,80,82,96,98,112,114,128,130,144,146,160,16..., dimensions={0} | all-to-all | bytes 294912 | tf_op jit(solution)/shard_map/all_to_all | solution.py:347
  75.9 0.1 total.1
  76.0 4.4 %collective-permute-start.1 = (f32[1,576]{1,0:T(1,128)S(1)}, f32[1,576]{1,0:T(1,128)S(1)}, u32[]{:S(2)}, u32[]{:S(2)}) collective-permute-start(f32[1,576]{1,0:T(1,128)S(1)} %total.1), channel_id=1, source_target_pairs={{0,0},{16,16},{32,32},{48,48},{64,1},{80,17},{96,33},{112,49},{2,2... | collective-permute-start | bytes 6920 | tf_op jit(solution)/shard_map/ppermute | solution.py:358
  80.4 7.4 %collective-permute-done.1 = f32[1,576]{1,0:T(1,128)S(1)} collective-permute-done((f32[1,576]{1,0:T(1,128)S(1)}, f32[1,576]{1,0:T(1,128)S(1)}, u32[]{:S(2)}, u32[]{:S(2)}) %collective-permute-start.1) | collective-permute-done | bytes 2336 | tf_op jit(solution)/shard_map/ppermute | solution.py:358
  87.8 1.4 %multiply_subtract_fusion = (f32[1,288]{1,0:T(1,128)}, f32[1,288]{1,0:T(1,128)}, f32[1,288]{1,0:T(1,128)}, f32[1,288]{1,0:T(1,128)}) fusion(f32[1,9216]{1,0:T(1,128)} %param.17, s32[]{:T(128)S(6)} %select_n.4, f32[1,576]{1,0:T(1,128)S(1)} %collective-permute-done.1, f32[1,9216]{1,0:T(1,128)} %param.16), kind=kLoop, calls=%fused_computation.3 | loop fusion | flops 2304 | bytes 9220 | tf_op jit(solution)/shard_map/sub | solution.py:366
  (5 shorter events, 0.0 us)
Async XLA Ops:
  0.6 0.7 copy-start.7
  1.3 0.9 %copy-start = (bf16[2,6,1,9216]{3,0,2,1:T(2,128)(2,1)S(1)}, bf16[2,6,1,9216]{3,0,2,1:T(2,128)(2,1)}, u32[]{:S(2)}) copy-start(bf16[2,6,1,9216]{3,0,2,1:T(2,128)(2,1)} %param.9) | copy-start | bytes 663556
  2.2 0.8 copy-start.1
  3.0 0.8 copy-start.2
  3.8 0.8 copy-start.3
  5.4 14.4 %collective-permute-start = (bf16[8,12288]{1,0:T(8,128)(2,1)S(1)}, bf16[8,12288]{1,0:T(8,128)(2,1)S(1)}, u32[]{:S(2)}, u32[]{:S(2)}) collective-permute-start(bf16[8,12288]{1,0:T(8,128)(2,1)S(1)} %get-tuple-element.7), channel_id=1, source_target_pairs={{0,2},{1,3},{2,0},{3,1},{4,6},{5,7},{6,4},{7,5},{8,10},{9,11},{10,... | collective-permute-start | bytes 589832 | tf_op jit(solution)/shard_map/ppermute | solution.py:334
  19.9 19.8 %copy-start.4 = (f32[16,9]{1,0:T(8,128)S(1)}, f32[16,9]{1,0:T(8,128)}, u32[]{:S(2)}) copy-start(f32[16,9]{1,0:T(8,128)} %coef_ref.1) | copy-start | bytes 1732
  19.9 19.7 %copy-start.6 = (f32[192]{0:T(256)S(1)}, f32[192]{0:T(256)}, u32[]{:S(2)}) copy-start(f32[192]{0:T(256)} %occupation_ref.1) | copy-start | bytes 2308
  39.6 0.7 copy-start.5
  39.6 0.7 copy-start.8
  76.0 11.8 %collective-permute-start.1 = (f32[1,576]{1,0:T(1,128)S(1)}, f32[1,576]{1,0:T(1,128)S(1)}, u32[]{:S(2)}, u32[]{:S(2)}) collective-permute-start(f32[1,576]{1,0:T(1,128)S(1)} %total.1), channel_id=1, source_target_pairs={{0,0},{16,16},{32,32},{48,48},{64,1},{80,17},{96,33},{112,49},{2,2... | collective-permute-start | bytes 6920 | tf_op jit(solution)/shard_map/ppermute | solution.py:358

commit v5 on v4

--- a/solution.py
+++ b/solution.py
@@ -30,9 +30,25 @@
 
 
 def pack_kernel(
-    quasi_ref, index_ref, mean_ref, pairing_ref, table_ref, mine_ref, theirs_ref, rows_ref, pot_ref
+    quasi_hbm, index_hbm, mean_hbm, pairing_hbm, table_ref, out_ref,
+    quasi_ref, index_ref, mean_ref, pairing_ref, rows_ref, pot_ref, sems,
 ):
-    half = (lax.axis_index("slab") // 2) % 2
+    pairs = (
+        (index_hbm, index_ref), (mean_hbm, mean_ref), (pairing_hbm, pairing_ref), (quasi_hbm, quasi_ref)
+    )
+    copies = [
+        pltpu.make_async_copy(source, target, sems.at[k]) for k, (source, target) in enumerate(pairs)
+    ]
+    for copy in copies:
+        copy.start()
+    for window, quads in ((0, (0, 1)), (WINDOWS - 1, (SPAN - 2, SPAN - 1))):
+        for group in range(2):
+            for quad in quads:
+                out_ref[slab_of(group, window), :, quad * QUAD : (quad + 1) * QUAD] = jnp.zeros(
+                    (8, QUAD), jnp.bfloat16
+                )
+    copies[0].wait()
+    copies[1].wait()
     index = index_ref[...]
     looked = jnp.zeros(index.shape, jnp.float32)
     for level in range(table_ref.shape[0]):
@@ -41,15 +57,18 @@
     high = potential.astype(jnp.bfloat16).astype(jnp.float32)
     pot_ref[0] = high
     pot_ref[1] = potential - high
-    for side, group in ((0, half), (1, 1 - half)):
+    for tile in range(TILES):
+        lanes = slice(tile * LANES, (tile + 1) * LANES)
+        for group in range(2):
+            rows_ref[group, 3:4, lanes] = pot_ref[0, tile : tile + 1, :]
+            rows_ref[group, 7:8, lanes] = pot_ref[1, tile : tile + 1, :]
+    copies[2].wait()
+    copies[3].wait()
+    for group in range(2):
         for slot in range(3):
             pair = quasi_ref[3 * group + slot].astype(jnp.float32)
-            rows_ref[side, slot : slot + 1, :] = pair[0:1]
-            rows_ref[side, 4 + slot : 5 + slot, :] = pair[1:2]
-        for tile in range(TILES):
-            lanes = slice(tile * LANES, (tile + 1) * LANES)
-            rows_ref[side, 3:4, lanes] = pot_ref[0, tile : tile + 1, :]
-            rows_ref[side, 7:8, lanes] = pot_ref[1, tile : tile + 1, :]
+            rows_ref[group, slot : slot + 1, :] = pair[0:1]
+            rows_ref[group, 4 + slot : 5 + slot, :] = pair[1:2]
     for quad in range(QUADS):
         first = 3 * quad
         values = jnp.concatenate(
@@ -57,32 +76,14 @@
         )
         upper = values.astype(jnp.bfloat16).astype(jnp.float32)
         extra = jnp.concatenate([upper, values - upper], axis=0).astype(jnp.bfloat16)
-        start = quad * QUAD
-        for side, out_ref in ((0, mine_ref), (1, theirs_ref)):
-            out_ref[:, start : start + 3 * LANES] = rows_ref[
-                side, :, first * LANES : (first + 3) * LANES
-            ].astype(jnp.bfloat16)
-            out_ref[:, start + 3 * LANES : start + QUAD] = extra
-
-
-def window_kernel(mine_ref, got_ref, out_ref):
-    half = (lax.axis_index("slab") // 2) % 2
-    for window in range(WINDOWS):
-        first = 3 * window - 2
-        begin, end = max(first, 0), min(first + SPAN, QUADS)
-        before, after = begin - first, first + SPAN - end
-        for ref, place in ((mine_ref, half), (got_ref, 1 - half)):
-            if before:
-                out_ref[window, place, :, : before * QUAD] = jnp.zeros(
-                    (8, before * QUAD), jnp.bfloat16
-                )
-            if after:
-                out_ref[window, place, :, (SPAN - after) * QUAD :] = jnp.zeros(
-                    (8, after * QUAD), jnp.bfloat16
-                )
-            out_ref[window, place, :, before * QUAD : (SPAN - after) * QUAD] = ref[
-                :, begin * QUAD : end * QUAD
-            ]
+        for group in range(2):
+            vectors = rows_ref[group, :, first * LANES : (first + 3) * LANES].astype(jnp.bfloat16)
+            for window in range(WINDOWS):
+                place = quad - (3 * window - 2)
+                if 0 <= place < SPAN:
+                    slab, start = slab_of(group, window), place * QUAD
+                    out_ref[slab, :, start : start + 3 * LANES] = vectors
+                    out_ref[slab, :, start + 3 * LANES : start + QUAD] = extra
 
 
 ROWS = 28
@@ -114,8 +115,7 @@
     def chosen(count, pick):
         out = lax.broadcasted_iota(jnp.int32, (count, LANES), 0)
         source = lax.broadcasted_iota(jnp.int32, (count, LANES), 1)
-        chip, core, half = source // 32, (source // 16) % 2, (source // 8) % 2
-        same = (out % PLANES) == 4 * chip + 2 * half + core
+        same = (out % PLANES) == (source // 8)
         return jnp.where(same & pick(out // PLANES, source % 8), 1.0, 0.0).astype(jnp.bfloat16)
 
     gather = chosen(
@@ -286,10 +286,6 @@
     )(message.reshape(8 * PLANES, SPAN * QUAD), counts, slot_slice, occupation, filter_coef)
 
 
-def window_groups():
-    return [[slab_of(group, window) for window in range(WINDOWS)] for group in range(2)]
-
-
 def summing_groups():
     return [
         [cut * 16 + slab_of(group, window) for cut in range(32) for group in range(2)]
@@ -313,16 +309,20 @@
 ):
     share = mean_field.shape[1] // lax.axis_size("cuts")
     packed = jnp.transpose(quasi, (1, 2, 0, 3)).reshape(CAP, 2, TILES * LANES)
-    mine, theirs = pl.pallas_call(
+    message = pl.pallas_call(
         pack_kernel,
-        out_shape=[jax.ShapeDtypeStruct((8, QUADS * QUAD), jnp.bfloat16)] * 2,
-        in_specs=vmem(4) + smem(1),
-        out_specs=vmem(2),
+        out_shape=jax.ShapeDtypeStruct((PLANES, 8, SPAN * QUAD), jnp.bfloat16),
+        in_specs=[pl.BlockSpec(memory_space=pltpu.HBM)] * 4 + smem(1),
+        out_specs=pl.BlockSpec(memory_space=pltpu.VMEM),
         scratch_shapes=[
+            pltpu.VMEM((CAP, 2, TILES * LANES), jnp.bfloat16),
+            pltpu.VMEM((TILES, LANES), jnp.int32),
+            pltpu.VMEM((TILES, LANES), jnp.float32),
+            pltpu.VMEM((TILES, LANES), jnp.float32),
             pltpu.VMEM((2, 8, TILES * LANES), jnp.float32),
             pltpu.VMEM((2, TILES, LANES), jnp.float32),
+            pltpu.SemaphoreType.DMA((4,)),
         ],
-        compiler_params=grant(8),
         name="pack",
     )(
         packed,
@@ -331,18 +331,7 @@
         pairing.reshape(TILES, LANES),
         trap_table,
     )
-    got = lax.ppermute(theirs, "slab", [(slab, slab ^ 2) for slab in range(16)])
-    message = pl.pallas_call(
-        window_kernel,
-        out_shape=jax.ShapeDtypeStruct((WINDOWS, 2, 8, SPAN * QUAD), jnp.bfloat16),
-        in_specs=vmem(2),
-        out_specs=pl.BlockSpec(memory_space=pltpu.VMEM),
-        compiler_params=grant(8),
-        name="window",
-    )(mine, got)
-    message = lax.all_to_all(
-        message, "slab", 0, 0, axis_index_groups=window_groups(), tiled=True
-    )
+    message = lax.all_to_all(message, "slab", 0, 0, tiled=True)
     parts = filter_call(message, counts, slot_slice, occupation, filter_coef)
     parts = lax.all_to_all(
         parts, ("cuts", "slab"), 0, 0, axis_index_groups=summing_groups(), tiled=True

time: 89.6 us -> 86.2 us (0.962)
  blocking collectives: 48.7 us -> 61.6 us
  starting transfers between devices: 12.1 us -> 3.99 us
  waiting for transfers between devices: 14.1 us -> 7.79 us
  local copies, waits for them, and re-layouts: 4.57 us -> 0.68 us
  Pallas kernels: 7.63 us -> 9.81 us
    all_to_all x1, blocking collectives: 19.7 us -> 30.2 us  [body(): message = lax.all_to_all(message, 'slab', 0, 0, tiled=True)]
    ppermute x1 -> x0, starting transfers between devices: 7.73 us -> none  [body(): got = lax.ppermute(theirs, 'slab', [(slab, slab ^ 2) for slab in range(16)])]
    ppermute x1 -> x0, waiting for transfers between devices: 6.7 us -> none  [body(): got = lax.ppermute(theirs, 'slab', [(slab, slab ^ 2) for slab in range(16)])]
    unnamed x18 -> x8, local copies, waits for them, and re-layouts: 4.57 us -> 0.68 us
    all_to_all x1, blocking collectives: 28.9 us -> 31.4 us  [body(): lax.all_to_all(parts, ('cuts', 'slab'), 0, 0, axis_index_groups=summing_g...]
    pallas_call x2 -> x1, Pallas kernels: 0.91 us -> 2.79 us  [body(): pl.pallas_call(pack_kernel, out_shape=jax.ShapeDtypeStruct((PLANES, 8, SP...]
  transfers between devices with their start and end apart: 2 -> 1, of which waited for: 2 -> 1; matrix products, arithmetic and copies ran while one was open for 0% -> 0% of each run, Pallas kernels for 0% -> 0%
where the time goes in v5:
time: 86.2 us; the launch traced here: 85.9 us
  blocking collectives  61.6 us (71%)
  Pallas kernels  9.81 us (11%)
  waiting for transfers between devices  7.79 us (9%)
  starting transfers between devices  3.99 us (5%)
  other arithmetic  1.35 us (2%)
    all_to_all x1, blocking collectives, body(): lax.all_to_all(parts, ('cuts', 'slab'), 0, 0, axis_index_groups=summing_g...  31.4 us
    all_to_all x1, blocking collectives, body(): message = lax.all_to_all(message, 'slab', 0, 0, tiled=True)  30.2 us
    ppermute x1, waiting for transfers between devices, body(): sums = lax.ppermute(sums, ('cuts', 'slab'), routes())  7.79 us
    pallas_call x1, Pallas kernels, filter_call(): pl.pallas_call(filter_kernel, out_shape=jax.ShapeDtypeStruct((64, 1, 2 *...  6.91 us
    ppermute x1, starting transfers between devices, body(): sums = lax.ppermute(sums, ('cuts', 'slab'), routes())  3.99 us
    pallas_call x1, Pallas kernels, body(): pl.pallas_call(pack_kernel, out_shape=jax.ShapeDtypeStruct((PLANES, 8, SP...  2.79 us
  transfers between devices with their start and end apart: 1, of which 1 were waited for; matrix products, arithmetic and copies ran while one was open for 0% of the time, Pallas kernels for 0%

profile of v5, /device:TPU:4, one launch (start us, length us, event | category | flops | bytes accessed | tf_op | source)
XLA Modules:
  0.0 85.9 jit_solution(9078671058148240465)
XLA Ops:
  0.6 2.8 %pack.1 = bf16[16,8,3584]{2,1,0:T(8,128)(2,1)} custom-call(bf16[6,2,9216]{2,1,0:T(2,128)(2,1)} %bitcast.10, s32[72,128]{1,0:T(8,128)} %bitcast.13, f32[72,128]{1,0:T(8,128)} %bitcast.12, f32[72,128]{1,0:T(8,128)} %bitcast.11, f32[32]{0:T(128)} %table_ref.1), custom_call_target="tpu_custom_call" | custom-call | tf_op jit(solution)/shard_map/pack/pallas_call | solution.py:312
  3.4 0.0 copy-start
  3.4 0.0 copy-start.2
  3.5 30.2 %all_to_all.10 = bf16[16,8,3584]{2,1,0:T(8,128)(2,1)S(1)} all-to-all(bf16[16,8,3584]{2,1,0:T(8,128)(2,1)} %pack.1), channel_id=1, replica_groups=mesh['cuts'=32,'slab'=16] {'slab'}, dimensions={0} | all-to-all | bytes 1835008 | tf_op jit(solution)/shard_map/all_to_all | solution.py:334
  33.6 0.0 copy-start.1
  33.6 0.0 copy-start.3
  33.6 0.0 copy-done
  33.6 0.0 copy-done.2
  33.6 0.7 copy-done.1
  34.3 0.0 copy-done.3
  34.3 6.9 %filter.1 = f32[64,1,576]{2,1,0:T(1,128)S(1)} custom-call(bf16[128,3584]{1,0:T(8,128)(2,1)S(1)} %bitcast.9, s32[32]{0:T(128)S(1)} %copy-done.3, s32[192]{0:T(256)S(1)} %copy-done.1, f32[192]{0:T(256)S(1)} %copy-done.2, f32[16,9]{1,0:T(8,128)S(1)} %copy-done), custom_call_target="tpu_custom_call" | custom-call | tf_op jit(solution)/shard_map/filter/pallas_call | solution.py:271
  41.2 31.4 %all_to_all.11.parts_ref = f32[64,1,576]{2,1,0:T(1,128)S(1)} all-to-all(f32[64,1,576]{2,1,0:T(1,128)S(1)} %filter.1), channel_id=1, replica_groups={{0,2,16,18,32,34,48,50,64,66,80,82,96,98,112,114,128,130,144,146,160,16..., dimensions={0} | all-to-all | bytes 294912 | tf_op jit(solution)/shard_map/all_to_all | solution.py:336
  72.6 0.1 total.1
  72.8 4.0 %collective-permute-start = (f32[1,576]{1,0:T(1,128)S(1)}, f32[1,576]{1,0:T(1,128)S(1)}, u32[]{:S(2)}, u32[]{:S(2)}) collective-permute-start(f32[1,576]{1,0:T(1,128)S(1)} %total.1), channel_id=1, source_target_pairs={{0,0},{16,16},{32,32},{48,48},{64,1},{80,17},{96,33},{112,49},{2,2... | collective-permute-start | bytes 6920 | tf_op jit(solution)/shard_map/ppermute | solution.py:347
  76.8 7.8 %collective-permute-done = f32[1,576]{1,0:T(1,128)S(1)} collective-permute-done((f32[1,576]{1,0:T(1,128)S(1)}, f32[1,576]{1,0:T(1,128)S(1)}, u32[]{:S(2)}, u32[]{:S(2)}) %collective-permute-start) | collective-permute-done | bytes 2336 | tf_op jit(solution)/shard_map/ppermute | solution.py:347
  84.6 1.4 %multiply_subtract_fusion = (f32[1,288]{1,0:T(1,128)}, f32[1,288]{1,0:T(1,128)}, f32[1,288]{1,0:T(1,128)}, f32[1,288]{1,0:T(1,128)}) fusion(f32[1,9216]{1,0:T(1,128)} %param.17, s32[]{:T(128)S(6)} %select_n.4, f32[1,576]{1,0:T(1,128)S(1)} %collective-permute-done, f32[1,9216]{1,0:T(1,128)} %param.16), kind=kLoop, calls=%fused_computation.3 | loop fusion | flops 2304 | bytes 9220 | tf_op jit(solution)/shard_map/sub | solution.py:355
Async XLA Ops:
  3.4 30.2 %copy-start = (f32[16,9]{1,0:T(8,128)S(1)}, f32[16,9]{1,0:T(8,128)}, u32[]{:S(2)}) copy-start(f32[16,9]{1,0:T(8,128)} %coef_ref.1) | copy-start | bytes 1732
  3.4 30.2 %copy-start.2 = (f32[192]{0:T(256)S(1)}, f32[192]{0:T(256)}, u32[]{:S(2)}) copy-start(f32[192]{0:T(256)} %occupation_ref.1) | copy-start | bytes 2308
  33.6 0.7 copy-start.1
  33.6 0.7 copy-start.3
  72.8 11.8 %collective-permute-start = (f32[1,576]{1,0:T(1,128)S(1)}, f32[1,576]{1,0:T(1,128)S(1)}, u32[]{:S(2)}, u32[]{:S(2)}) collective-permute-start(f32[1,576]{1,0:T(1,128)S(1)} %total.1), channel_id=1, source_target_pairs={{0,0},{16,16},{32,32},{48,48},{64,1},{80,17},{96,33},{112,49},{2,2... | collective-permute-start | bytes 6920 | tf_op jit(solution)/shard_map/ppermute | solution.py:347

commit v6 on v3

--- a/solution.py
+++ b/solution.py
@@ -207,14 +207,26 @@
 
     lax.fori_loop(0, 3, vector, 0)
 
-    for density in range(2):
-        for y in range(OWN):
-            lanes = slice((3 * density + y % 3) * LANES, (3 * density + y % 3 + 1) * LANES)
-            at = (density * OWN + y) * 16
-            for high in range(2):
-                values = density_ref[at + 8 * high : at + 8 * high + 8, :]
-                for k in range(8):
-                    out_ref[piece_of(8 * high + k, y // 3), :, lanes] = values[k : k + 1]
+    for quarter in range(4):
+        for high in range(2):
+            at = 48 * quarter + 8 * high
+            normal = [density_ref[at + 16 * k : at + 16 * k + 8, :] for k in range(3)]
+            at = at + OWN * 16
+            other = [density_ref[at + 16 * k : at + 16 * k + 8, :] for k in range(3)]
+            second, third = pltpu.roll(normal[1], 96, 1), pltpu.roll(normal[2], 64, 1)
+            last = pltpu.roll(other[2], 96, 1)
+            tiles = [
+                jnp.where(lane < 96, normal[0], second),
+                jnp.where(lane < 64, second, third),
+                jnp.where(lane < 32, third, pltpu.roll(other[0], 32, 1)),
+                jnp.where(lane < 96, other[1], last),
+                last[:, :64],
+            ]
+            for k in range(8):
+                piece = piece_of(8 * high + k, quarter)
+                for tile, values in enumerate(tiles):
+                    lanes = slice(tile * LANES, tile * LANES + values.shape[1])
+                    out_ref[piece, :, lanes] = values[k : k + 1]
 
 
 def piece_of(plane, quarter):
@@ -223,17 +235,7 @@
 
 
 def sum_kernel(parts_ref, out_ref):
-    total = jnp.sum(parts_ref[...], axis=0)
-    lane = lax.broadcasted_iota(jnp.int32, (1, LANES), 1)
-    for density in range(2):
-        first, second, third = [
-            total[:, (3 * density + k) * LANES : (3 * density + k + 1) * LANES] for k in range(3)
-        ]
-        second, third = pltpu.roll(second, 96, 1), pltpu.roll(third, 64, 1)
-        row = slice(density, density + 1)
-        out_ref[row, 0:128] = jnp.where(lane < 96, first, second)
-        out_ref[row, 128:256] = jnp.where(lane < 64, second, third)
-        out_ref[row, 256:288] = third[:, :32]
+    out_ref[...] = jnp.sum(parts_ref[...], axis=0)
 
 
 def vmem(count):
@@ -242,13 +244,17 @@
 
 def smem(count):
     return [pl.BlockSpec(memory_space=pltpu.SMEM)] * count
+
+
+def grant(mebibytes):
+    return pltpu.CompilerParams(vmem_limit_bytes=mebibytes << 20)
 
 
 def filter_call(low, own, high, counts, slot_slice, occupation, filter_coef):
     flat = [part.reshape(8 * PLANES, part.shape[2]) for part in (low, own, high)]
     return pl.pallas_call(
         filter_kernel,
-        out_shape=jax.ShapeDtypeStruct((64, 1, 6 * LANES), jnp.float32),
+        out_shape=jax.ShapeDtypeStruct((64, 1, 2 * 288), jnp.float32),
         in_specs=vmem(3) + smem(4),
         out_specs=pl.BlockSpec(memory_space=pltpu.VMEM),
         scratch_shapes=[
@@ -259,6 +265,7 @@
             pltpu.VMEM((2 * OWN * 16, LANES), jnp.float32),
             pltpu.VMEM((2 * OWN * 16, LANES), jnp.float32),
         ],
+        compiler_params=grant(16),
         name="filter",
     )(*flat, counts, slot_slice, occupation, filter_coef)
 
@@ -321,17 +328,18 @@
     )
     sums = pl.pallas_call(
         sum_kernel,
-        out_shape=jax.ShapeDtypeStruct((2, 288), jnp.float32),
+        out_shape=jax.ShapeDtypeStruct((1, 2 * 288), jnp.float32),
         in_specs=vmem(1),
         out_specs=pl.BlockSpec(memory_space=pltpu.VMEM),
+        compiler_params=grant(4),
         name="total",
     )(parts)
     sums = lax.ppermute(sums, ("cuts", "slab"), routes())
     offset = lax.axis_index("cuts") * share
     mean_local = lax.dynamic_slice_in_dim(mean_field, offset, share, 1)
     pairing_local = lax.dynamic_slice_in_dim(pairing, offset, share, 1)
-    normal_density = sums[0:1]
-    anomalous_density = sums[1:2]
+    normal_density = sums[:, :share]
+    anomalous_density = sums[:, share:]
     cube_root = jnp.cbrt(normal_density + density_floor)
     new_mean_field = 0.5 * mean_local + 0.5 * (beta_coef * cube_root * cube_root - chem_level)
     new_pairing = 0.5 * pairing_local - coupling * anomalous_density

time: 87.7 us -> 83.4 us (0.951)
  Pallas kernels: 11.4 us -> 8.73 us
    pallas_call x2, Pallas kernels: 9.4 us -> 6.71 us  [the longest x1 6.6 us: filter_call(): pl.pallas_call(filter_kernel, out_shape=jax.ShapeDtypeStruct((64, 1, 2 *...]
where the time goes in v6:
time: 83.4 us; the launch traced here: 83 us
  blocking collectives  49.9 us (60%)
  waiting for transfers between devices  15.4 us (18%)
  Pallas kernels  8.73 us (10%)
  starting transfers between devices  6.24 us (7%)
  other arithmetic  1.35 us (2%)
    all_to_all x1, blocking collectives, body(): lax.all_to_all(parts, ('cuts', 'slab'), 0, 0, axis_index_groups=summing_g...  27.1 us
    all_to_all x1, blocking collectives, body(): message = lax.all_to_all(message, 'slab', 0, 0, tiled=True)  22.7 us
    ppermute x1, waiting for transfers between devices, body(): sums = lax.ppermute(sums, ('cuts', 'slab'), routes())  9.86 us
    pallas_call x1, Pallas kernels, filter_call(): pl.pallas_call(filter_kernel, out_shape=jax.ShapeDtypeStruct((64, 1, 2 *...  6.6 us
    ppermute x1, waiting for transfers between devices, body(): low = lax.ppermute(message[:, :, MESSAGE - HALO:], 'slab', neighbours(1))  3.82 us
    ppermute x1, starting transfers between devices, body(): high = lax.ppermute(message[:, :, :HALO], 'slab', neighbours(-1))  2.22 us
    ppermute x1, starting transfers between devices, body(): low = lax.ppermute(message[:, :, MESSAGE - HALO:], 'slab', neighbours(1))  2.11 us
    pallas_call x1, Pallas kernels, body(): pl.pallas_call(pack_kernel, out_shape=jax.ShapeDtypeStruct((PLANES, 8, ME...  2.01 us
  transfers between devices with their start and end apart: 3, of which 3 were waited for; matrix products, arithmetic and copies ran while one was open for 0% of the time, Pallas kernels for 0%

profile of v6, /device:TPU:4, one launch (start us, length us, event | category | flops | bytes accessed | tf_op | source)
XLA Modules:
  0.0 83.0 jit_solution(8524800899922705074)
XLA Ops:
  0.6 2.0 %pack.1 = bf16[16,8,1536]{2,1,0:T(8,128)(2,1)} custom-call(bf16[6,2,9216]{2,1,0:T(2,128)(2,1)} %bitcast.14, s32[72,128]{1,0:T(8,128)} %bitcast.17, f32[72,128]{1,0:T(8,128)} %bitcast.16, f32[72,128]{1,0:T(8,128)} %bitcast.15, f32[32]{0:T(128)} %table_ref.1), custom_call_target="tpu_custom_call" | custom-call | tf_op jit(solution)/shard_map/pack/pallas_call | solution.py:305
  2.6 22.7 %all_to_all.10 = bf16[16,8,1536]{2,1,0:T(8,128)(2,1)S(1)} all-to-all(bf16[16,8,1536]{2,1,0:T(8,128)(2,1)} %pack.1), channel_id=1, replica_groups=mesh['cuts'=32,'slab'=16] {'slab'}, dimensions={0} | all-to-all | bytes 786432 | tf_op jit(solution)/shard_map/all_to_all | solution.py:322
  25.4 0.0 copy-start.2
  25.4 0.0 copy-start.3
  25.4 0.0 copy-start
  25.5 2.2 %collective-permute-start.1 = (bf16[16,8,1024]{2,1,0:T(8,128)(2,1)S(1)}, bf16[16,8,1024]{2,1,0:T(8,128)(2,1)S(1)}, u32[]{:S(2)}, u32[]{:S(2)}) collective-permute-start(bf16[16,8,1024]{2,1,0:T(8,128)(2,1)S(1)} %get-tuple-element.8), channel_id=1, source_target_pairs={{1,0},{4,1},{5,4},{8,5},{9,8},{12,9},{13,12},{3,2},{6,3},{7,6},{10... | collective-permute-start | bytes 786440 | tf_op jit(solution)/shard_map/ppermute | solution.py:324
  27.7 2.1 %collective-permute-start = (bf16[16,8,1024]{2,1,0:T(8,128)(2,1)S(1)}, bf16[16,8,1024]{2,1,0:T(8,128)(2,1)S(1)}, u32[]{:S(2)}, u32[]{:S(2)}) collective-permute-start(bf16[16,8,1024]{2,1,0:T(8,128)(2,1)S(1)} %get-tuple-element.9), channel_id=1, source_target_pairs={{0,1},{1,4},{4,5},{5,8},{8,9},{9,12},{12,13},{2,3},{3,6},{6,7},{7,... | collective-permute-start | bytes 786440 | tf_op jit(solution)/shard_map/ppermute | solution.py:323
  29.8 1.8 %collective-permute-done.1 = bf16[16,8,1024]{2,1,0:T(8,128)(2,1)S(1)} collective-permute-done((bf16[16,8,1024]{2,1,0:T(8,128)(2,1)S(1)}, bf16[16,8,1024]{2,1,0:T(8,128)(2,1)S(1)}, u32[]{:S(2)}, u32[]{:S(2)}) %collective-permute-start.1) | collective-permute-done | bytes 262176 | tf_op jit(solution)/shard_map/ppermute | solution.py:324
  31.5 3.8 %collective-permute-done = bf16[16,8,1024]{2,1,0:T(8,128)(2,1)S(1)} collective-permute-done((bf16[16,8,1024]{2,1,0:T(8,128)(2,1)S(1)}, bf16[16,8,1024]{2,1,0:T(8,128)(2,1)S(1)}, u32[]{:S(2)}, u32[]{:S(2)}) %collective-permute-start) | collective-permute-done | bytes 262176 | tf_op jit(solution)/shard_map/ppermute | solution.py:323
  35.4 0.0 copy-start.1
  35.4 0.0 copy-done.2
  35.4 0.0 copy-done.3
  35.4 0.0 copy-done
  35.4 0.7 copy-done.1
  36.0 6.6 %filter.1 = f32[64,1,576]{2,1,0:T(1,128)S(1)} custom-call(bf16[128,1024]{1,0:T(8,128)(2,1)S(1)} %bitcast.13, bf16[128,1536]{1,0:T(8,128)(2,1)S(1)} %bitcast.11, bf16[128,1024]{1,0:T(8,128)(2,1)S(1)} %bitcast.12, s32[32]{0:T(128)S(1)} %copy-done.3, s32[192]{0:T(256)S(1)} %copy-done.1, f32[192]{0:T(256)S(1)} %copy-done.2, f32[16,9]{1,0:T(8,128)S(1)} %copy-done), custom_call_target="tpu_custom_call" | custom-call | tf_op jit(solution)/shard_map/filter/pallas_call | solution.py:255
  42.7 27.1 %all_to_all.11.parts_ref = f32[64,1,576]{2,1,0:T(1,128)S(1)} all-to-all(f32[64,1,576]{2,1,0:T(1,128)S(1)} %filter.1), channel_id=1, replica_groups={{0,2,16,18,32,34,48,50,64,66,80,82,96,98,112,114,128,130,144,146,160,16..., dimensions={0} | all-to-all | bytes 294912 | tf_op jit(solution)/shard_map/all_to_all | solution.py:326
  69.8 0.1 total.1
  69.9 1.9 %collective-permute-start.2 = (f32[1,576]{1,0:T(1,128)S(1)}, f32[1,576]{1,0:T(1,128)S(1)}, u32[]{:S(2)}, u32[]{:S(2)}) collective-permute-start(f32[1,576]{1,0:T(1,128)S(1)} %total.1), channel_id=1, source_target_pairs={{0,0},{16,16},{32,32},{48,48},{64,1},{80,17},{96,33},{112,49},{2,2... | collective-permute-start | bytes 6920 | tf_op jit(solution)/shard_map/ppermute | solution.py:337
  71.8 9.9 %collective-permute-done.2 = f32[1,576]{1,0:T(1,128)S(1)} collective-permute-done((f32[1,576]{1,0:T(1,128)S(1)}, f32[1,576]{1,0:T(1,128)S(1)}, u32[]{:S(2)}, u32[]{:S(2)}) %collective-permute-start.2) | collective-permute-done | bytes 2336 | tf_op jit(solution)/shard_map/ppermute | solution.py:337
  81.7 1.4 %multiply_subtract_fusion = (f32[1,288]{1,0:T(1,128)}, f32[1,288]{1,0:T(1,128)}, f32[1,288]{1,0:T(1,128)}, f32[1,288]{1,0:T(1,128)}) fusion(f32[1,9216]{1,0:T(1,128)} %param.17, s32[]{:T(128)S(6)} %select_n.4, f32[1,576]{1,0:T(1,128)S(1)} %collective-permute-done.2, f32[1,9216]{1,0:T(1,128)} %param.16), kind=kLoop, calls=%fused_computation.3 | loop fusion | flops 2304 | bytes 9220 | tf_op jit(solution)/shard_map/sub | solution.py:345
  (1 shorter events, 0.0 us)
Async XLA Ops:
  25.4 10.0 %copy-start.2 = (f32[192]{0:T(256)S(1)}, f32[192]{0:T(256)}, u32[]{:S(2)}) copy-start(f32[192]{0:T(256)} %occupation_ref.1) | copy-start | bytes 2308
  25.4 10.0 %copy-start.3 = (s32[32]{0:T(128)S(1)}, s32[32]{0:T(128)}, u32[]{:S(2)}) copy-start(s32[32]{0:T(128)} %counts_ref.1) | copy-start | bytes 388
  25.4 9.9 %copy-start = (f32[16,9]{1,0:T(8,128)S(1)}, f32[16,9]{1,0:T(8,128)}, u32[]{:S(2)}) copy-start(f32[16,9]{1,0:T(8,128)} %coef_ref.1) | copy-start | bytes 1732
  25.5 6.1 %collective-permute-start.1 = (bf16[16,8,1024]{2,1,0:T(8,128)(2,1)S(1)}, bf16[16,8,1024]{2,1,0:T(8,128)(2,1)S(1)}, u32[]{:S(2)}, u32[]{:S(2)}) collective-permute-start(bf16[16,8,1024]{2,1,0:T(8,128)(2,1)S(1)} %get-tuple-element.8), channel_id=1, source_target_pairs={{1,0},{4,1},{5,4},{8,5},{9,8},{12,9},{13,12},{3,2},{6,3},{7,6},{10... | collective-permute-start | bytes 786440 | tf_op jit(solution)/shard_map/ppermute | solution.py:324
  27.7 7.7 %collective-permute-start = (bf16[16,8,1024]{2,1,0:T(8,128)(2,1)S(1)}, bf16[16,8,1024]{2,1,0:T(8,128)(2,1)S(1)}, u32[]{:S(2)}, u32[]{:S(2)}) collective-permute-start(bf16[16,8,1024]{2,1,0:T(8,128)(2,1)S(1)} %get-tuple-element.9), channel_id=1, source_target_pairs={{0,1},{1,4},{4,5},{5,8},{8,9},{9,12},{12,13},{2,3},{3,6},{6,7},{7,... | collective-permute-start | bytes 786440 | tf_op jit(solution)/shard_map/ppermute | solution.py:323
  35.4 0.7 copy-start.1
  69.9 11.8 %collective-permute-start.2 = (f32[1,576]{1,0:T(1,128)S(1)}, f32[1,576]{1,0:T(1,128)S(1)}, u32[]{:S(2)}, u32[]{:S(2)}) collective-permute-start(f32[1,576]{1,0:T(1,128)S(1)} %total.1), channel_id=1, source_target_pairs={{0,0},{16,16},{32,32},{48,48},{64,1},{80,17},{96,33},{112,49},{2,2... | collective-permute-start | bytes 6920 | tf_op jit(solution)/shard_map/ppermute | solution.py:337

commit v7 on v6

--- a/solution.py
+++ b/solution.py
@@ -29,7 +29,30 @@
     return (window // 2) * 4 + group * 2 + window % 2
 
 
-def pack_kernel(quasi_ref, index_ref, mean_ref, pairing_ref, table_ref, out_ref, rows_ref, pot_ref):
+def pack_kernel(
+    quasi_hbm, index_hbm, mean_hbm, pairing_hbm, table_ref, counts_ref, slice_ref, occupation_ref, coef_ref,
+    out_ref, terms_ref,
+    quasi_ref, index_ref, mean_ref, pairing_ref, rows_ref, pot_ref, sems,
+):
+    pairs = (
+        (index_hbm, index_ref), (mean_hbm, mean_ref), (pairing_hbm, pairing_ref), (quasi_hbm, quasi_ref)
+    )
+    copies = [
+        pltpu.make_async_copy(source, target, sems.at[k]) for k, (source, target) in enumerate(pairs)
+    ]
+    for copy in copies:
+        copy.start()
+    cut = lax.axis_index("cuts")
+    half = (lax.axis_index("slab") // 2) % 2
+    live = counts_ref[cut]
+    for slot in range(3):
+        place = half * 3 + slot
+        which = slice_ref[cut * CAP + place]
+        for order in range(DEGREE + 1):
+            terms_ref[16 * slot + order] = coef_ref[which, order]
+        terms_ref[16 * slot + 9] = jnp.where(place < live, occupation_ref[cut * CAP + place], 0.0)
+    for copy in copies:
+        copy.wait()
     index = index_ref[...]
     looked = jnp.zeros(index.shape, jnp.float32)
     for level in range(table_ref.shape[0]):
@@ -71,12 +94,10 @@
 
 
 def filter_kernel(
-    low_ref, own_ref, high_ref, counts_ref, slice_ref, occupation_ref, coef_ref, out_ref,
+    low_ref, own_ref, high_ref, terms_ref, out_ref,
     one_ref, two_ref, a_ref, c_ref, acc_ref, density_ref,
 ):
-    cut = lax.axis_index("cuts")
     slab = lax.axis_index("slab")
-    group = (slab // 2) % 2
     window = (slab // 4) * 2 + slab % 2
     scale = 2.0 / spectral_scale
     lane = lax.broadcasted_iota(jnp.int32, (8, LANES), 1)
@@ -145,13 +166,9 @@
                 a_ref[at, :] = (rows[k][96 + 8 * high : 104 + 8 * high] + 3.0) * (mask * scale)
                 c_ref[at, :] = pairs[k][8 * high : 8 * high + 8] * (mask * scale)
 
-    live = counts_ref[cut]
-    start = cut * CAP + group * 3
-
     def vector(slot, carry):
-        which = slice_ref[start + slot]
-        weight = jnp.where(group * 3 + slot < live, occupation_ref[start + slot], 0.0)
-        coefs = [coef_ref[which, order] for order in range(DEGREE + 1)]
+        coefs = [terms_ref[16 * slot + order] for order in range(DEGREE + 1)]
+        weight = terms_ref[16 * slot + 9]
         shift = slot * BLOCK
 
         def load(ref, comp, y, offset):
@@ -250,12 +267,12 @@
     return pltpu.CompilerParams(vmem_limit_bytes=mebibytes << 20)
 
 
-def filter_call(low, own, high, counts, slot_slice, occupation, filter_coef):
+def filter_call(low, own, high, terms):
     flat = [part.reshape(8 * PLANES, part.shape[2]) for part in (low, own, high)]
     return pl.pallas_call(
         filter_kernel,
         out_shape=jax.ShapeDtypeStruct((64, 1, 2 * 288), jnp.float32),
-        in_specs=vmem(3) + smem(4),
+        in_specs=vmem(3) + smem(1),
         out_specs=pl.BlockSpec(memory_space=pltpu.VMEM),
         scratch_shapes=[
             pltpu.VMEM((6 * BLOCK + 8, LANES), jnp.float32),
@@ -267,7 +284,7 @@
         ],
         compiler_params=grant(16),
         name="filter",
-    )(*flat, counts, slot_slice, occupation, filter_coef)
+    )(*flat, terms)
 
 
 def neighbours(by):
@@ -302,15 +319,24 @@
 ):
     share = mean_field.shape[1] // lax.axis_size("cuts")
     packed = jnp.transpose(quasi, (1, 2, 0, 3)).reshape(CAP, 2, TILES * LANES)
-    message = pl.pallas_call(
+    message, terms = pl.pallas_call(
         pack_kernel,
-        out_shape=jax.ShapeDtypeStruct((PLANES, 8, MESSAGE), jnp.bfloat16),
-        in_specs=vmem(4) + smem(1),
-        out_specs=pl.BlockSpec(memory_space=pltpu.VMEM),
+        out_shape=[
+            jax.ShapeDtypeStruct((PLANES, 8, MESSAGE), jnp.bfloat16),
+            jax.ShapeDtypeStruct((64,), jnp.float32),
+        ],
+        in_specs=[pl.BlockSpec(memory_space=pltpu.HBM)] * 4 + smem(5),
+        out_specs=vmem(1) + smem(1),
         scratch_shapes=[
+            pltpu.VMEM((CAP, 2, TILES * LANES), jnp.bfloat16),
+            pltpu.VMEM((TILES, LANES), jnp.int32),
+            pltpu.VMEM((TILES, LANES), jnp.float32),
+            pltpu.VMEM((TILES, LANES), jnp.float32),
             pltpu.VMEM((2, 8, TILES * LANES), jnp.float32),
             pltpu.VMEM((2, TILES, LANES), jnp.float32),
+            pltpu.SemaphoreType.DMA((4,)),
         ],
+        compiler_params=pltpu.CompilerParams(vmem_limit_bytes=66500000),
         name="pack",
     )(
         packed,
@@ -318,11 +344,15 @@
         mean_field.reshape(TILES, LANES),
         pairing.reshape(TILES, LANES),
         trap_table,
+        counts,
+        slot_slice,
+        occupation,
+        filter_coef,
     )
     message = lax.all_to_all(message, "slab", 0, 0, tiled=True)
     low = lax.ppermute(message[:, :, MESSAGE - HALO :], "slab", neighbours(1))
     high = lax.ppermute(message[:, :, :HALO], "slab", neighbours(-1))
-    parts = filter_call(low, message, high, counts, slot_slice, occupation, filter_coef)
+    parts = filter_call(low, message, high, terms)
     parts = lax.all_to_all(
         parts, ("cuts", "slab"), 0, 0, axis_index_groups=summing_groups(), tiled=True
     )

time: 83.4 us -> 84.4 us (1.012)
  waiting for transfers between devices: 15.4 us -> 13.7 us
  starting transfers between devices: 6.24 us -> 7.48 us
    ppermute x1, waiting for transfers between devices: 3.82 us -> 2.11 us  [body(): low = lax.ppermute(message[:, :, MESSAGE - HALO:], 'slab', neighbours(1))]
    ppermute x1, starting transfers between devices: 2.22 us -> 3.64 us  [body(): high = lax.ppermute(message[:, :, :HALO], 'slab', neighbours(-1))]
    pallas_call x1, Pallas kernels: 2.01 us -> 2.94 us  [body(): pl.pallas_call(pack_kernel, out_shape=[jax.ShapeDtypeStruct((PLANES, 8, M...]
where the time goes in v7:
time: 84.4 us; the launch traced here: 84 us
  blocking collectives  50.6 us (60%)
  waiting for transfers between devices  13.7 us (16%)
  Pallas kernels  9.49 us (11%)
  starting transfers between devices  7.48 us (9%)
  other arithmetic  1.35 us (2%)
    all_to_all x1, blocking collectives, body(): lax.all_to_all(parts, ('cuts', 'slab'), 0, 0, axis_index_groups=summing_g...  27.8 us
    all_to_all x1, blocking collectives, body(): message = lax.all_to_all(message, 'slab', 0, 0, tiled=True)  22.8 us
    ppermute x1, waiting for transfers between devices, body(): sums = lax.ppermute(sums, ('cuts', 'slab'), routes())  9.86 us
    pallas_call x1, Pallas kernels, filter_call(): pl.pallas_call(filter_kernel, out_shape=jax.ShapeDtypeStruct((64, 1, 2 *...  6.43 us
    ppermute x1, starting transfers between devices, body(): high = lax.ppermute(message[:, :, :HALO], 'slab', neighbours(-1))  3.64 us
    pallas_call x1, Pallas kernels, body(): pl.pallas_call(pack_kernel, out_shape=[jax.ShapeDtypeStruct((PLANES, 8, M...  2.94 us
    ppermute x1, waiting for transfers between devices, body(): low = lax.ppermute(message[:, :, MESSAGE - HALO:], 'slab', neighbours(1))  2.11 us
    ppermute x1, starting transfers between devices, body(): low = lax.ppermute(message[:, :, MESSAGE - HALO:], 'slab', neighbours(1))  1.92 us
  transfers between devices with their start and end apart: 3, of which 3 were waited for; matrix products, arithmetic and copies ran while one was open for 0% of the time, Pallas kernels for 0%

profile of v7, /device:TPU:4, one launch (start us, length us, event | category | flops | bytes accessed | tf_op | source)
XLA Modules:
  0.0 84.0 jit_solution(6121693468421585948)
XLA Ops:
  0.6 2.9 %pack.1 = (bf16[16,8,1536]{2,1,0:T(8,128)(2,1)}, f32[64]{0:T(128)}) custom-call(bf16[6,2,9216]{2,1,0:T(2,128)(2,1)} %bitcast.14, s32[72,128]{1,0:T(8,128)} %bitcast.17, f32[72,128]{1,0:T(8,128)} %bitcast.16, f32[72,128]{1,0:T(8,128)} %bitcast.15, f32[32]{0:T(128)} %table_ref.1, s32[32]{0:T(128)} %counts_ref.1, s32[192]{0:T(256)} %slice_ref.1, ...), custom_call_target="tpu_custom_call" | custom-call | tf_op jit(solution)/shard_map/pack/pallas_call | solution.py:322
  3.6 22.8 %all_to_all.10 = bf16[16,8,1536]{2,1,0:T(8,128)(2,1)S(1)} all-to-all(bf16[16,8,1536]{2,1,0:T(8,128)(2,1)} %get-tuple-element.6), channel_id=1, replica_groups=mesh['cuts'=32,'slab'=16] {'slab'}, dimensions={0} | all-to-all | bytes 786432 | tf_op jit(solution)/shard_map/all_to_all | solution.py:352
  26.4 1.9 %collective-permute-start = (bf16[16,8,1024]{2,1,0:T(8,128)(2,1)S(1)}, bf16[16,8,1024]{2,1,0:T(8,128)(2,1)S(1)}, u32[]{:S(2)}, u32[]{:S(2)}) collective-permute-start(bf16[16,8,1024]{2,1,0:T(8,128)(2,1)S(1)} %get-tuple-element.13), channel_id=1, source_target_pairs={{0,1},{1,4},{4,5},{5,8},{8,9},{9,12},{12,13},{2,3},{3,6},{6,7},{7,... | collective-permute-start | bytes 786440 | tf_op jit(solution)/shard_map/ppermute | solution.py:353
  28.3 3.6 %collective-permute-start.1 = (bf16[16,8,1024]{2,1,0:T(8,128)(2,1)S(1)}, bf16[16,8,1024]{2,1,0:T(8,128)(2,1)S(1)}, u32[]{:S(2)}, u32[]{:S(2)}) collective-permute-start(bf16[16,8,1024]{2,1,0:T(8,128)(2,1)S(1)} %get-tuple-element.12), channel_id=1, source_target_pairs={{1,0},{4,1},{5,4},{8,5},{9,8},{12,9},{13,12},{3,2},{6,3},{7,6},{10... | collective-permute-start | bytes 786440 | tf_op jit(solution)/shard_map/ppermute | solution.py:354
  32.0 2.1 %collective-permute-done = bf16[16,8,1024]{2,1,0:T(8,128)(2,1)S(1)} collective-permute-done((bf16[16,8,1024]{2,1,0:T(8,128)(2,1)S(1)}, bf16[16,8,1024]{2,1,0:T(8,128)(2,1)S(1)}, u32[]{:S(2)}, u32[]{:S(2)}) %collective-permute-start) | collective-permute-done | bytes 262176 | tf_op jit(solution)/shard_map/ppermute | solution.py:353
  34.1 1.8 %collective-permute-done.1 = bf16[16,8,1024]{2,1,0:T(8,128)(2,1)S(1)} collective-permute-done((bf16[16,8,1024]{2,1,0:T(8,128)(2,1)S(1)}, bf16[16,8,1024]{2,1,0:T(8,128)(2,1)S(1)}, u32[]{:S(2)}, u32[]{:S(2)}) %collective-permute-start.1) | collective-permute-done | bytes 262176 | tf_op jit(solution)/shard_map/ppermute | solution.py:354
  35.8 0.0 copy-start
  35.8 0.7 copy-done
  36.5 6.4 %filter.1 = f32[64,1,576]{2,1,0:T(1,128)S(1)} custom-call(bf16[128,1024]{1,0:T(8,128)(2,1)S(1)} %bitcast.12, bf16[128,1536]{1,0:T(8,128)(2,1)S(1)} %bitcast.11, bf16[128,1024]{1,0:T(8,128)(2,1)S(1)} %bitcast.13, f32[64]{0:T(128)S(1)} %copy-done), custom_call_target="tpu_custom_call" | custom-call | tf_op jit(solution)/shard_map/filter/pallas_call | solution.py:272
  42.9 27.8 %all_to_all.11.parts_ref = f32[64,1,576]{2,1,0:T(1,128)S(1)} all-to-all(f32[64,1,576]{2,1,0:T(1,128)S(1)} %filter.1), channel_id=1, replica_groups={{0,2,16,18,32,34,48,50,64,66,80,82,96,98,112,114,128,130,144,146,160,16..., dimensions={0} | all-to-all | bytes 294912 | tf_op jit(solution)/shard_map/all_to_all | solution.py:356
  70.8 0.1 total.1
  70.9 1.9 %collective-permute-start.2 = (f32[1,576]{1,0:T(1,128)S(1)}, f32[1,576]{1,0:T(1,128)S(1)}, u32[]{:S(2)}, u32[]{:S(2)}) collective-permute-start(f32[1,576]{1,0:T(1,128)S(1)} %total.1), channel_id=1, source_target_pairs={{0,0},{16,16},{32,32},{48,48},{64,1},{80,17},{96,33},{112,49},{2,2... | collective-permute-start | bytes 6920 | tf_op jit(solution)/shard_map/ppermute | solution.py:367
  72.8 9.9 %collective-permute-done.2 = f32[1,576]{1,0:T(1,128)S(1)} collective-permute-done((f32[1,576]{1,0:T(1,128)S(1)}, f32[1,576]{1,0:T(1,128)S(1)}, u32[]{:S(2)}, u32[]{:S(2)}) %collective-permute-start.2) | collective-permute-done | bytes 2336 | tf_op jit(solution)/shard_map/ppermute | solution.py:367
  82.7 1.4 %multiply_subtract_fusion = (f32[1,288]{1,0:T(1,128)}, f32[1,288]{1,0:T(1,128)}, f32[1,288]{1,0:T(1,128)}, f32[1,288]{1,0:T(1,128)}) fusion(f32[1,9216]{1,0:T(1,128)} %param.17, s32[]{:T(128)S(6)} %select_n.4, f32[1,576]{1,0:T(1,128)S(1)} %collective-permute-done.2, f32[1,9216]{1,0:T(1,128)} %param.16), kind=kLoop, calls=%fused_computation.3 | loop fusion | flops 2304 | bytes 9220 | tf_op jit(solution)/shard_map/sub | solution.py:375
  (1 shorter events, 0.0 us)
Async XLA Ops:
  26.4 7.7 %collective-permute-start = (bf16[16,8,1024]{2,1,0:T(8,128)(2,1)S(1)}, bf16[16,8,1024]{2,1,0:T(8,128)(2,1)S(1)}, u32[]{:S(2)}, u32[]{:S(2)}) collective-permute-start(bf16[16,8,1024]{2,1,0:T(8,128)(2,1)S(1)} %get-tuple-element.13), channel_id=1, source_target_pairs={{0,1},{1,4},{4,5},{5,8},{8,9},{9,12},{12,13},{2,3},{3,6},{6,7},{7,... | collective-permute-start | bytes 786440 | tf_op jit(solution)/shard_map/ppermute | solution.py:353
  28.3 7.5 %collective-permute-start.1 = (bf16[16,8,1024]{2,1,0:T(8,128)(2,1)S(1)}, bf16[16,8,1024]{2,1,0:T(8,128)(2,1)S(1)}, u32[]{:S(2)}, u32[]{:S(2)}) collective-permute-start(bf16[16,8,1024]{2,1,0:T(8,128)(2,1)S(1)} %get-tuple-element.12), channel_id=1, source_target_pairs={{1,0},{4,1},{5,4},{8,5},{9,8},{12,9},{13,12},{3,2},{6,3},{7,6},{10... | collective-permute-start | bytes 786440 | tf_op jit(solution)/shard_map/ppermute | solution.py:354
  35.8 0.7 copy-start
  70.9 11.8 %collective-permute-start.2 = (f32[1,576]{1,0:T(1,128)S(1)}, f32[1,576]{1,0:T(1,128)S(1)}, u32[]{:S(2)}, u32[]{:S(2)}) collective-permute-start(f32[1,576]{1,0:T(1,128)S(1)} %total.1), channel_id=1, source_target_pairs={{0,0},{16,16},{32,32},{48,48},{64,1},{80,17},{96,33},{112,49},{2,2... | collective-permute-start | bytes 6920 | tf_op jit(solution)/shard_map/ppermute | solution.py:367
